TPU v7x, 256 devices: a whole 4x4x8 slice. The times are simulated.
256 devices in a mesh: grp: 8 (over x_lo, y), smp: 32 (over x_hi, z, core).
Axes of the slice: x: 4 (x_hi: 2, x_lo: 2; x = x_hi * 2 + x_lo), y: 4, z: 8, core: 2. Of those that a mesh axis runs over, the one named last changes fastest.
Arguments:
- spins_packed: int32 [32, 32768], P(None, 'smp'), may hold values from -2147483648 to 2147483646
- weight: bfloat16 [1024, 8192], P(None, 'grp'), may hold values from -0.1875 to 0.1875
- hidden_bias: float32 [8192], P('grp'), may hold values from -1.5 to 1.5
- force_w: float32 [1024, 8192], P('smp', 'grp'), may hold values from -6 to 6
- force_b: float32 [8192], P('grp'), may hold values from -6 to 6
Outputs:
- update_w: float32 [1024, 8192], P('smp', 'grp')
- update_b: float32 [8192], P('grp')
All inputs are finite; a program needn't handle non-finite values.
Results may differ from a plain program's by a relative error of at most 0.0003.
Values sent between devices are 32-bit elements; how exact they have to be, the bound alone decides.
A program may use at most 64 MiB of HBM per device.

v0:
```python
import functools

import jax
import jax.numpy as jnp
from jax import lax
from jax.experimental import pallas as pl
from jax.experimental.pallas import tpu as pltpu
from jax.sharding import PartitionSpec as P

MESH = pl.DeviceIdType.MESH
F32, BF16 = jnp.float32, jnp.bfloat16
diag_shift = 0.01
EXTRA = 128
PAD = 16


def total(x):
    return jnp.sum(jnp.sum(x, axis=0, keepdims=True), axis=1, keepdims=True)


def kernel(
    groups, shards,
    packed_ref, weight_ref, bias_ref, force_ref, force_b_ref,
    out_ref, out_b_ref,
    packed, weight_t, bias_t, tile, spins, hidden, force_other, lhs, scaled,
    image, image_other, residual, residual_b, by_group, by_shard,
    packed_send, packed_recv, force_sem, image_send, image_recv,
    group_send, group_recv, shard_send, shard_recv,
):
    grp, smp = lax.axis_index("grp"), lax.axis_index("smp")
    chips = shards // 2
    core, chip = lax.rem(smp, 2), smp // 2
    sibling = smp + 1 - 2 * core
    words, here = packed_ref.shape
    units, rows = weight_ref.shape[1], force_ref.shape[0]
    pair = 2 * rows
    samples = chips * here
    count = samples * 2
    block = hidden_block = min(512, units)
    part = image.shape[2]
    parts = units // part

    barrier = pltpu.get_barrier_semaphore()
    for step in range(1, groups):
        pl.semaphore_signal(barrier, device_id={"grp": lax.rem(grp + step, groups)}, device_id_type=MESH)
    for step in range(1, shards):
        pl.semaphore_signal(barrier, device_id={"smp": lax.rem(smp + step, shards)}, device_id_type=MESH)
    pl.semaphore_wait(barrier, groups + shards - 2)

    packed_copies = []
    for step in range(1, chips):
        peer = lax.rem(chip + step, chips)
        packed_copies.append(
            pltpu.make_async_remote_copy(
                packed_ref, packed.at[chip], packed_send.at[step], packed_recv.at[chip],
                device_id={"smp": 2 * peer + core}, device_id_type=MESH,
            )
        )
        packed_copies[-1].start()
    force_copy = pltpu.make_async_remote_copy(
        force_ref, force_other, force_sem.at[0], force_sem.at[1],
        device_id={"smp": sibling}, device_id_type=MESH,
    )
    force_copy.start()
    packed[chip] = packed_ref[...]

    def turn(at, carry):
        cols = pl.ds(pl.multiple_of(at * 256, 256), 256)
        weight_t[cols, :] = weight_ref[:, cols].T
        bias_t[cols, :] = jnp.broadcast_to(bias_ref[:, cols], (128, 256)).T
        return carry

    lax.fori_loop(0, units // 256, turn, 0)

    def own_rows(of):
        return pl.ds(pl.multiple_of(of * rows, rows), rows)

    zero_rows = jnp.zeros((PAD - 1, units), F32)
    lhs[pl.ds(pair, PAD), :] = jnp.concatenate([force_b_ref[...] / chips, zero_rows], axis=0).astype(BF16)
    lhs[own_rows(core), :] = force_ref[...].astype(BF16)
    force_copy.wait()
    lhs[own_rows(1 - core), :] = force_other[...].astype(BF16)

    shifts = lax.broadcasted_iota(jnp.int32, (32, block), 0)
    tiles = here // block

    def values_of(cols):
        projected = jnp.dot(lhs[...], hidden[:, cols], preferred_element_type=F32)
        value = jnp.sum(projected[:pair] * spins[:, cols].astype(F32), axis=0, keepdims=True)
        return value + projected[pair : pair + 1]

    def hidden_block_of(at_chip, turn_at, carry):
        local = pl.ds(pl.multiple_of(turn_at * block, block), block)
        cols = pl.ds(pl.multiple_of(at_chip * here + turn_at * block, block), block)
        for word in range(words):
            bits = jnp.right_shift(jnp.broadcast_to(packed[at_chip, word : word + 1, local], (32, block)), shifts)
            tile[word * 32 : word * 32 + 32, :] = (2 * jnp.bitwise_and(bits, 1) - 1).astype(F32).astype(BF16)
        spins[:, cols] = tile[pl.ds(pl.multiple_of(chip * pair, pair), pair), :]
        for unit in range(0, units, hidden_block):
            these = pl.ds(unit, hidden_block)
            pre = jnp.dot(weight_t[these, :], tile[...], preferred_element_type=F32)
            bias = bias_t[these, :]
            pre = pre + jnp.concatenate([bias] * (block // 128), axis=1)
            hidden[these, cols] = jnp.tanh(pre).astype(BF16)
        by_group[0, grp, :, cols] = values_of(cols)
        return carry

    for step in range(chips):
        at_chip = lax.rem(chip + chips - step, chips)
        if step:
            pltpu.make_async_remote_copy(
                packed_ref, packed.at[at_chip], packed_send.at[step], packed_recv.at[at_chip],
                device_id={"smp": sibling}, device_id_type=MESH,
            ).wait_recv()
        lax.fori_loop(0, tiles, functools.partial(hidden_block_of, at_chip), 0)
    for copy in packed_copies:
        copy.wait_send()

    def gather(slots, which, axis, size, me, send, recv):
        copies = []
        for step in range(1, size):
            copies.append(
                pltpu.make_async_remote_copy(
                    slots.at[which, me], slots.at[which, me], send.at[which, step], recv.at[which, me],
                    device_id={axis: lax.rem(me + step, size)}, device_id_type=MESH,
                )
            )
            copies[-1].start()
        for step in range(1, size):
            source = lax.rem(me + size - step, size)
            pltpu.make_async_remote_copy(
                slots.at[which, source], slots.at[which, source], send.at[which, step], recv.at[which, source],
                device_id={axis: source}, device_id_type=MESH,
            ).wait_recv()
        for copy in copies:
            copy.wait_send()

    lane = lax.broadcasted_iota(jnp.int32, (1, EXTRA), 1)

    def reduce_values(which, first, second):
        by_group[which, grp, :, samples:] = jnp.where(lane == 0, first, jnp.where(lane == 1, second, 0.0))
        gather(by_group, which, "grp", groups, grp, group_send, group_recv)
        mine = by_group[which, 0]
        for source in range(1, groups):
            mine = mine + by_group[which, source]
        by_shard[which, smp] = mine
        gather(by_shard, which, "smp", shards, smp, shard_send, shard_recv)
        halves = []
        for half in range(2):
            value = by_shard[which, half]
            for source in range(half + 2, shards, 2):
                value = value + by_shard[which, source]
            halves.append(value)
        extra = halves[0][:, samples:] + halves[1][:, samples:]
        first = jnp.sum(jnp.where(lane == 0, extra, 0.0), axis=1, keepdims=True)
        second = jnp.sum(jnp.where(lane == 1, extra, 0.0), axis=1, keepdims=True)
        return halves[0][:, :samples], halves[1][:, :samples], first, second

    def centre(low, high):
        mean = total(low) / count + total(high) / count
        return low - mean, high - mean

    force_dot = total(force_ref[...] * force_ref[...]) + total(force_b_ref[...] * force_b_ref[...]) / shards
    low0, high0, norm0, _ = reduce_values(0, force_dot, jnp.zeros((1, 1), F32))
    low, high = centre(low0, high0)
    curvature0 = total(low * low) / count + total(high * high) / count + diag_shift * norm0
    step0 = norm0 / curvature0

    mine = (jnp.where(core == 0, low, high)).astype(F32)
    for at in range(0, samples, block):
        weights = mine[:, at : at + block]
        scaled[:pair, at : at + block] = (spins[:, at : at + block].astype(F32) * weights).astype(BF16)
        scaled[pair:, at : at + block] = jnp.concatenate(
            [weights, jnp.zeros((PAD - 1, block), F32)], axis=0
        ).astype(BF16)

    def image_copy(at):
        return pltpu.make_async_remote_copy(
            image.at[at], image_other.at[at], image_send.at[at], image_recv.at[at],
            device_id={"smp": sibling}, device_id_type=MESH,
        )

    def image_part(at, carry):
        these = pl.ds(pl.multiple_of(at * part, part), part)
        image[at] = lax.dot_general(
            scaled[...], hidden[these, :], (((1,), (1,)), ((), ())), preferred_element_type=F32
        )
        image_copy(at).start()
        return carry

    lax.fori_loop(0, parts, image_part, 0)

    scale = 1.0 / count

    def residual_part(at, carry):
        first, second = carry
        these = pl.ds(pl.multiple_of(at * part, part), part)
        image_copy(at).wait()

        def next_residual(which, force):
            whole = image[at, which, :] + image_other[at, which, :]
            return force - step0 * (whole * scale + diag_shift * force)

        own = next_residual(own_rows(core), force_ref[:, these])
        residual[:, these] = own
        lhs[own_rows(core), these] = own.astype(BF16)
        lhs[own_rows(1 - core), these] = next_residual(own_rows(1 - core), force_other[:, these]).astype(BF16)
        own_b = next_residual(pl.ds(pair, 1), force_b_ref[:, these])
        residual_b[:, these] = own_b
        lhs[pl.ds(pair, PAD), these] = jnp.concatenate([own_b / chips, jnp.zeros((PAD - 1, part), F32)], axis=0).astype(BF16)
        first = first + total(own * own) + total(own_b * own_b) / shards
        second = second + total(own * force_ref[:, these]) + total(own_b * force_b_ref[:, these]) / shards
        return first, second

    zero = jnp.zeros((1, 1), F32)
    own_norm, own_cross = lax.fori_loop(0, parts, residual_part, (zero, zero))

    def second_values(at, carry):
        cols = pl.ds(pl.multiple_of(at * block, block), block)
        by_group[1, grp, :, cols] = values_of(cols)
        return carry

    lax.fori_loop(0, samples // block, second_values, 0)
    low1, high1, norm1, cross = reduce_values(1, own_norm, own_cross)
    beta = norm1 / norm0
    low, high = centre(low1 + beta * low0, high1 + beta * high0)
    direction_dot = norm1 + 2.0 * beta * cross + beta * beta * norm0
    curvature1 = total(low * low) / count + total(high * high) / count + diag_shift * direction_dot
    step1 = norm1 / curvature1

    out_ref[...] = step0 * force_ref[...] + step1 * (residual[...] + beta * force_ref[...])
    out_b_ref[...] = step0 * force_b_ref[...] + step1 * (residual_b[...] + beta * force_b_ref[...])


def body(groups, shards, spins_packed, weight, hidden_bias, force_w, force_b):
    words, here = spins_packed.shape
    inputs, units = weight.shape
    rows = force_w.shape[0]
    chips = shards // 2
    samples, pair = chips * here, 2 * rows
    part = 256
    parts = units // part
    vmem = pl.BlockSpec(memory_space=pltpu.VMEM)
    dma = pltpu.SemaphoreType.DMA
    update_w, update_b = pl.pallas_call(
        functools.partial(kernel, groups, shards),
        out_shape=(jax.ShapeDtypeStruct((rows, units), F32), jax.ShapeDtypeStruct((1, units), F32)),
        in_specs=[vmem] * 5,
        out_specs=(vmem, vmem),
        scratch_shapes=[
            pltpu.VMEM((chips, words, here), jnp.int32),
            pltpu.VMEM((units, inputs), BF16),
            pltpu.VMEM((units, 128), F32),
            pltpu.VMEM((inputs, min(512, units)), BF16),
            pltpu.VMEM((pair, samples), BF16),
            pltpu.VMEM((units, samples), BF16),
            pltpu.VMEM((rows, units), F32),
            pltpu.VMEM((pair + PAD, units), BF16),
            pltpu.VMEM((pair + PAD, samples), BF16),
            pltpu.VMEM((parts, pair + PAD, part), F32),
            pltpu.VMEM((parts, pair + PAD, part), F32),
            pltpu.VMEM((rows, units), F32),
            pltpu.VMEM((1, units), F32),
            pltpu.VMEM((2, groups, 1, samples + EXTRA), F32),
            pltpu.VMEM((2, shards, 1, samples + EXTRA), F32),
            dma((chips,)),
            dma((chips,)),
            dma((2,)),
            dma((parts,)),
            dma((parts,)),
            dma((2, groups)),
            dma((2, groups)),
            dma((2, shards)),
            dma((2, shards)),
        ],
        compiler_params=pltpu.CompilerParams(
            collective_id=0, has_side_effects=True, vmem_limit_bytes=62 * 1024 * 1024
        ),
    )(spins_packed, weight, hidden_bias.reshape(1, -1), force_w, force_b.reshape(1, -1))
    return update_w, update_b.reshape(-1)


def solution(mesh):
    placed = (P(None, "smp"), P(None, "grp"), P("grp"), P("smp", "grp"), P("grp"))
    return jax.shard_map(
        functools.partial(body, mesh.shape["grp"], mesh.shape["smp"]),
        mesh=mesh, in_specs=placed, out_specs=(P("smp", "grp"), P("grp")), check_vma=False,
    )
```

profile of v0, /device:TPU:1, one launch (start us, length us, event | category | flops | bytes accessed | tf_op | source)
XLA Modules:
  0.0 221.2 jit_solution(3213612637027593778)
XLA Ops:
  0.6 217.7 %shard_map.68 = (f32[32,1024]{1,0:T(8,128)}, f32[1,1024]{1,0:T(1,128)}) custom-call(s32[32,1024]{1,0:T(8,128)} %packed_ref.1, bf16[1024,1024]{1,0:T(8,128)(2,1)} %weight_ref.1, f32[1,1024]{1,0:T(1,128)} %bitcast.3, f32[32,1024]{1,0:T(8,128)} %force_ref.1, f32[1,1024]{1,0:T(1,128)} %bitcast.4), custom_call_target="tpu_custom_call" | custom-call | tf_op jit(solution)/shard_map/pallas_call | solution.py:245
  218.4 1.6 copy.9
  219.9 1.3 copy.10
where the time goes:
time: 221 us
  Pallas kernels  218 us (99%)
  local copies, waits for them, and re-layouts  2.85 us (1%)
    pallas_call x1, Pallas kernels, body(): pl.pallas_call(functools.partial(kernel, groups, shards), out_shape=(jax....  218 us

commit v1 on v0

v1 whole, which is shorter than its diff:
```python
import functools

import jax
import jax.numpy as jnp
from jax import lax
from jax.experimental import pallas as pl
from jax.experimental.pallas import tpu as pltpu
from jax.sharding import PartitionSpec as P

MESH = pl.DeviceIdType.MESH
F32, BF16 = jnp.float32, jnp.bfloat16
diag_shift = 0.01
SETS = 8
EXTRA = 256
PAD = 16
PART = 256


def total(x):
    return jnp.sum(jnp.sum(x, axis=0, keepdims=True), axis=1, keepdims=True)


def kernel(
    groups, ranks,
    packed_ref, weight_ref, bias_ref, force_ref, force_b_ref,
    out_ref, out_b_ref,
    packed, weight_t, bias_t, tile, spins, hidden, force_all, lhs, scaled,
    image, image_core, image_z, image_x, image_all, image_b, by_group, by_rank, by_set,
    spin_send, spin_recv, force_send, force_recv, image_send, image_recv, sum_send, sum_recv,
    group_send, group_recv, rank_send, rank_recv, set_send, set_recv, bias_send, bias_recv,
):
    grp, smp = lax.axis_index("grp"), lax.axis_index("smp")
    words, here = packed_ref.shape
    inputs, units = weight_ref.shape
    rows = force_ref.shape[0]
    pair = SETS * rows
    samples = ranks * here
    count = samples * SETS
    block = min(512, here)
    parts = units // PART
    depth = 2 * ranks

    core, z, half = lax.rem(smp, 2), lax.rem(smp // 2, depth), smp // (2 * depth)
    parity, rank = lax.rem(z, 2), z // 2
    member = (core * 2 + parity) * 2 + half

    def device(half_at, z_at, core_at):
        return {"smp": (half_at * depth + z_at) * 2 + core_at}

    sibling = device(half, z, 1 - core)
    z_partner = device(half, z + 1 - 2 * parity, core)
    x_partner = device(1 - half, z, core)

    def group_device(at):
        return {"grp": at}

    def rank_device(at):
        return device(half, 2 * at + parity, core)

    def set_device(at):
        return device(lax.rem(at, 2), 2 * rank + lax.rem(at // 2, 2), at // 4)

    def remote(source, target, send, recv, where):
        return pltpu.make_async_remote_copy(
            source, target, send, recv, device_id=where, device_id_type=MESH
        )

    with jax.named_scope("barrier"):
        barrier = pltpu.get_barrier_semaphore()
        for size, me, peer in ((groups, grp, group_device), (ranks, rank, rank_device), (SETS, member, set_device)):
            for step in range(1, size):
                pl.semaphore_signal(barrier, device_id=peer(lax.rem(me + step, size)), device_id_type=MESH)
        pl.semaphore_wait(barrier, groups + ranks + SETS - 3)

    after, before, across = lax.rem(rank + 1, ranks), lax.rem(rank + ranks - 1, ranks), lax.rem(rank + 2, ranks)
    split = words // 2

    def spin_copy(which):
        source, target, where = (
            (packed_ref, packed.at[rank], after),
            (packed_ref, packed.at[rank], before),
            (packed.at[before, pl.ds(0, split)], packed.at[before, pl.ds(0, split)], after),
            (packed.at[after, pl.ds(split, split)], packed.at[after, pl.ds(split, split)], before),
        )[which]
        return remote(source, target, spin_send.at[which], spin_recv.at[which], rank_device(where))

    def spin_arrival(which):
        target = (
            packed.at[before], packed.at[after],
            packed.at[across, pl.ds(0, split)], packed.at[across, pl.ds(split, split)],
        )[which]
        return remote(target, target, spin_send.at[which], spin_recv.at[which], sibling)

    def share(slots, send, recv):
        def own(at, source):
            for which, where in ((1, x_partner), (0, z_partner)):
                remote(source, slots.at[at, core, parity, half], send.at[at, which], recv.at[at, which], where).start()

        def arrived(at, which):
            target = (
                slots.at[at, core, 1 - parity, half],
                slots.at[at, core, parity, 1 - half],
                slots.at[at, core, 1 - parity, 1 - half],
                slots.at[at, 1 - core, parity],
                slots.at[at, 1 - core, 1 - parity],
            )[which]
            remote(target, target, send.at[at, which], recv.at[at, which], sibling).wait_recv()

        def after_x(at):
            arrived(at, 1)
            block_x = slots.at[at, core, parity, 1 - half]
            remote(block_x, block_x, send.at[at, 2], recv.at[at, 2], z_partner).start()
            ours = slots.at[at, core, parity]
            remote(ours, ours, send.at[at, 3], recv.at[at, 3], sibling).start()

        def after_z(at):
            arrived(at, 0)
            arrived(at, 2)
            theirs = slots.at[at, core, 1 - parity]
            remote(theirs, theirs, send.at[at, 4], recv.at[at, 4], sibling).start()

        def whole(at):
            arrived(at, 3)
            arrived(at, 4)

        def sent(at):
            for which in range(3):
                target = slots.at[at, core, parity, half]
                remote(target, target, send.at[at, which], recv.at[at, which], sibling).wait_send()
            for which in range(3, 5):
                target = slots.at[at, core, parity]
                remote(target, target, send.at[at, which], recv.at[at, which], sibling).wait_send()

        return own, after_x, after_z, whole, sent

    def each_part(step):
        def run(at, carry):
            step(at)
            return carry

        lax.fori_loop(0, parts, run, 0)

    def cols_of(at):
        return pl.ds(pl.multiple_of(at * PART, PART), PART)

    force_own, force_x, force_z, force_whole, force_sent = share(force_all, force_send, force_recv)
    for at in range(parts):
        force_own(at, force_ref.at[:, pl.ds(at * PART, PART)])
    spin_copy(0).start()
    spin_copy(1).start()

    packed[rank] = packed_ref[...]
    for at in range(parts):
        force_all[at, core, parity, half] = force_ref[:, at * PART : (at + 1) * PART]

    def turn(at, carry):
        cols = pl.ds(pl.multiple_of(at * 256, 256), 256)
        weight_t[cols, :] = weight_ref[:, cols].T
        bias_t[cols, :] = jnp.broadcast_to(bias_ref[:, cols], (128, 256)).T
        return carry

    with jax.named_scope("turn"):
        lax.fori_loop(0, units // 256, turn, 0)

    masks = jnp.left_shift(1, lax.broadcasted_iota(jnp.int32, (32, block), 0))

    def hidden_block(at_rank, at, carry):
        local = pl.ds(pl.multiple_of(at * block, block), block)
        cols = pl.ds(pl.multiple_of(at_rank * here + at * block, block), block)
        for word in range(words):
            bits = jnp.bitwise_and(jnp.broadcast_to(packed[at_rank, word : word + 1, local], (32, block)), masks)
            tile[word * 32 : word * 32 + 32, :] = jnp.where(bits != 0, 1.0, -1.0).astype(BF16)
        for to in range(SETS):
            word = (to % 2) * 2 * depth + 4 * rank + 2 * (to // 2 % 2) + to // 4
            spins[to * rows : (to + 1) * rows, cols] = tile[pl.ds(pl.multiple_of(word * rows, rows), rows), :]
        for unit in range(0, units, 512):
            these = pl.ds(unit, 512)
            pre = jnp.dot(weight_t[these, :], tile[...], preferred_element_type=F32)
            pre = pre + jnp.concatenate([bias_t[these, :]] * (block // 128), axis=1)
            hidden[these, cols] = jnp.tanh(pre).astype(BF16)
        return carry

    def hidden_of(at_rank):
        lax.fori_loop(0, here // block, functools.partial(hidden_block, at_rank), 0)

    with jax.named_scope("hidden0"):
        hidden_of(rank)
    with jax.named_scope("spinwait"):
        spin_arrival(0).wait_recv()
        spin_copy(2).start()
        spin_arrival(1).wait_recv()
        spin_copy(3).start()
    with jax.named_scope("hidden1"):
        hidden_of(before)
    with jax.named_scope("forcex"):
        each_part(force_x)
    with jax.named_scope("hidden2"):
        hidden_of(after)
    with jax.named_scope("forcez"):
        each_part(force_z)
        spin_arrival(2).wait_recv()
        spin_arrival(3).wait_recv()
    with jax.named_scope("hidden3"):
        hidden_of(across)
    with jax.named_scope("forcew"):
        each_part(force_whole)

    def fill_lhs(at, slots, row):
        cols = cols_of(at)
        for to in range(SETS):
            lhs[to * rows : (to + 1) * rows, cols] = slots[at, to // 4, to // 2 % 2, to % 2].astype(BF16)
        lhs[pair:, cols] = jnp.concatenate([row / ranks, jnp.zeros((PAD - 1, PART), F32)], axis=0).astype(BF16)

    each_part(lambda at: fill_lhs(at, force_all, force_b_ref[:, cols_of(at)]))

    def weighed(projected, cols):
        value = jnp.sum(projected[:pair] * spins[:, cols].astype(F32), axis=0, keepdims=True)
        return value + projected[pair : pair + 1]

    def first_values(at, carry):
        cols = pl.ds(pl.multiple_of(at * block, block), block)
        by_group[0, grp, :, cols] = weighed(jnp.dot(lhs[...], hidden[:, cols], preferred_element_type=F32), cols)
        return carry

    with jax.named_scope("values0"):
        lax.fori_loop(0, samples // block, first_values, 0)

    def gather(slot, size, me, peer, send, recv):
        copies = []
        for step in range(1, size):
            copies.append(remote(slot(me), slot(me), send.at[step], recv.at[me], peer(lax.rem(me + step, size))))
            copies[-1].start()

        def finish():
            for step in range(1, size):
                source = lax.rem(me + size - step, size)
                remote(slot(source), slot(source), send.at[step], recv.at[source], sibling).wait_recv()
            for copy in copies:
                copy.wait_send()

        return finish

    def wide(x, lanes):
        return jnp.broadcast_to(x, (1, lanes))

    def reduce_values(which, first, second):
        by_group[which, grp, :, samples:] = jnp.concatenate([wide(first, 128), wide(second, 128)], axis=1)
        with jax.named_scope("redg"):
            gather(lambda at: by_group.at[which, at], groups, grp, group_device, group_send.at[which], group_recv.at[which])()
            mine = by_group[which, 0]
            for source in range(1, groups):
                mine = mine + by_group[which, source]
        by_rank[which, rank] = mine
        with jax.named_scope("redr"):
            gather(lambda at: by_rank.at[which, at], ranks, rank, rank_device, rank_send.at[which], rank_recv.at[which])()
            whole = by_rank[which, 0]
            for source in range(1, ranks):
                whole = whole + by_rank[which, source]
        return whole[:, :samples], whole[:, samples : samples + 1], whole[:, samples + 128 : samples + 129]

    def gather_sets(which, values):
        fill = jnp.zeros((8 - len(values), 128), F32)
        by_set[which, member] = jnp.concatenate([wide(value, 128) for value in values] + [fill], axis=0)
        return gather(lambda at: by_set.at[which, at], SETS, member, set_device, set_send.at[which], set_recv.at[which])

    def set_sum(which, row):
        value = by_set[which, 0, row : row + 1, :]
        for source in range(1, SETS):
            value = value + by_set[which, source, row : row + 1, :]
        return value[:, :1]

    def moments(which, values, others):
        mean = total(values) / samples
        apart = values - mean
        with jax.named_scope("sets"):
            gather_sets(which, [mean, total(apart * apart)] + others)()
        middle = set_sum(which, 0) / SETS
        spread = jnp.zeros((1, 1), F32)
        for source in range(SETS):
            shift = by_set[which, source, 0:1, :1] - middle
            spread = spread + shift * shift
        return middle, (set_sum(which, 1) + samples * spread) / count

    force_dot = total(force_ref[...] * force_ref[...]) + total(force_b_ref[...] * force_b_ref[...]) / (ranks * SETS)
    values0, own_dot, _ = reduce_values(0, force_dot, jnp.zeros((1, 1), F32))
    mean0, variance0 = moments(0, values0, [own_dot])
    norm0 = set_sum(0, 2)
    step0 = norm0 / (variance0 + diag_shift * norm0)

    centred = values0 - mean0
    with jax.named_scope("scaled"):
        for at in range(0, samples, block):
            weights = centred[:, at : at + block]
            scaled[:pair, at : at + block] = (spins[:, at : at + block].astype(F32) * weights).astype(BF16)
            scaled[pair:, at : at + block] = jnp.concatenate(
                [weights, jnp.zeros((PAD - 1, block), F32)], axis=0
            ).astype(BF16)

    def core_copy(at):
        return remote(image.at[at, 1 - core], image_core.at[at], sum_send.at[at, 0], sum_recv.at[at, 0], sibling)

    def z_copy(at):
        return remote(image.at[at, core, 1 - parity], image_z.at[at], sum_send.at[at, 1], sum_recv.at[at, 1], z_partner)

    def x_copy(at):
        return remote(
            image.at[at, core, parity, 1 - half], image_x.at[at], sum_send.at[at, 2], sum_recv.at[at, 2], x_partner
        )

    def image_part(at):
        part = lax.dot_general(
            scaled[...], hidden[cols_of(at), :], (((1,), (1,)), ((), ())), preferred_element_type=F32
        )
        for to in range(SETS):
            image[at, to // 4, to // 2 % 2, to % 2] = part[to * rows : (to + 1) * rows]
        core_copy(at).start()
        image_b[member, :, cols_of(at)] = part[pair : pair + 1]

    image_own, gather_x, gather_z, gather_whole, gather_sent = share(image_all, image_send, image_recv)

    def sum_core(at):
        core_copy(at).wait_recv()
        image[at, core, 1 - parity] = image[at, core, 1 - parity] + image_core[at, 1 - parity]
        z_copy(at).start()
        image[at, core, parity] = image[at, core, parity] + image_core[at, parity]

    def sum_z(at):
        z_copy(at).wait_recv()
        image[at, core, parity, 1 - half] = image[at, core, parity, 1 - half] + image_z[at, 1 - half]
        x_copy(at).start()
        image[at, core, parity, half] = image[at, core, parity, half] + image_z[at, half]

    def sum_x(at):
        x_copy(at).wait_recv()
        image_all[at, core, parity, half] = image[at, core, parity, half] + image_x[at]
        image_own(at, image_all.at[at, core, parity, half])

    with jax.named_scope("image"):
        each_part(image_part)
    finish_bias = gather(lambda at: image_b.at[at], SETS, member, set_device, bias_send, bias_recv)
    with jax.named_scope("sumcore"):
        each_part(sum_core)
    with jax.named_scope("sumz"):
        each_part(sum_z)
    with jax.named_scope("sumx"):
        each_part(sum_x)

    keep = 1.0 - diag_shift * step0
    pull = step0 / count
    with jax.named_scope("bias"):
        finish_bias()
        whole_b = image_b[0]
        for source in range(1, SETS):
            whole_b = whole_b + image_b[source]
        residual_b = keep * force_b_ref[...] - pull * whole_b
        own_norm = total(residual_b * residual_b) / (ranks * SETS)
        own_cross = total(residual_b * force_b_ref[...]) / (ranks * SETS)
        for at in range(parts):
            force = force_ref[:, at * PART : (at + 1) * PART]
            residual = keep * force - pull * image_all[at, core, parity, half]
            own_norm = own_norm + total(residual * residual)
            own_cross = own_cross + total(residual * force)
        finish_norm = gather_sets(1, [own_norm, own_cross])
        image_b[0] = whole_b

    with jax.named_scope("gatherx"):
        each_part(gather_x)
    with jax.named_scope("gatherz"):
        each_part(gather_z)

    def second_values(at):
        gather_whole(at)
        fill_lhs(at, image_all, image_b[0, :, cols_of(at)])

        def run(to, carry):
            cols = pl.ds(pl.multiple_of(to * block, block), block)
            product = jnp.dot(lhs[:, cols_of(at)], hidden[cols_of(at), cols], preferred_element_type=F32)
            before_it = jnp.where(at == 0, 0.0, by_group[1, grp, :, cols])
            by_group[1, grp, :, cols] = before_it + weighed(product, cols)
            return carry

        lax.fori_loop(0, samples // block, run, 0)

    by_group[1, grp, :, :samples] = jnp.zeros((1, samples), F32)
    with jax.named_scope("values1"):
        each_part(second_values)
        finish_norm()
    image_values, norm1, cross = reduce_values(1, set_sum(1, 0), set_sum(1, 1))
    beta = norm1 / norm0
    _, variance1 = moments(2, (keep + beta) * values0 - pull * image_values, [])
    direction_dot = norm1 + 2.0 * beta * cross + beta * beta * norm0
    step1 = norm1 / (variance1 + diag_shift * direction_dot)

    for_force = step0 + step1 * (keep + beta)
    for_image = step1 * pull
    with jax.named_scope("out"):
        for at in range(parts):
            cols = slice(at * PART, (at + 1) * PART)
            out_ref[:, cols] = for_force * force_ref[:, cols] - for_image * image_all[at, core, parity, half]
        out_b_ref[...] = for_force * force_b_ref[...] - for_image * image_b[0]

        for which in range(4):
            spin_copy(which).wait_send()
        each_part(force_sent)
        each_part(gather_sent)

        def sums_sent(at):
            core_copy(at).wait_send()
            z_copy(at).wait_send()
            x_copy(at).wait_send()

        each_part(sums_sent)


def body(groups, shards, spins_packed, weight, hidden_bias, force_w, force_b):
    words, here = spins_packed.shape
    inputs, units = weight.shape
    rows = force_w.shape[0]
    ranks = shards // SETS
    samples, pair = ranks * here, SETS * rows
    parts = units // PART
    vmem = pl.BlockSpec(memory_space=pltpu.VMEM)
    dma = pltpu.SemaphoreType.DMA
    update_w, update_b = pl.pallas_call(
        functools.partial(kernel, groups, ranks),
        out_shape=(jax.ShapeDtypeStruct((rows, units), F32), jax.ShapeDtypeStruct((1, units), F32)),
        in_specs=[vmem] * 5,
        out_specs=(vmem, vmem),
        scratch_shapes=[
            pltpu.VMEM((ranks, words, here), jnp.int32),
            pltpu.VMEM((units, inputs), BF16),
            pltpu.VMEM((units, 128), F32),
            pltpu.VMEM((inputs, min(512, here)), BF16),
            pltpu.VMEM((pair, samples), BF16),
            pltpu.VMEM((units, samples), BF16),
            pltpu.VMEM((parts, 2, 2, 2, rows, PART), F32),
            pltpu.VMEM((pair + PAD, units), BF16),
            pltpu.VMEM((pair + PAD, samples), BF16),
            pltpu.VMEM((parts, 2, 2, 2, rows, PART), F32),
            pltpu.VMEM((parts, 2, 2, rows, PART), F32),
            pltpu.VMEM((parts, 2, rows, PART), F32),
            pltpu.VMEM((parts, rows, PART), F32),
            pltpu.VMEM((parts, 2, 2, 2, rows, PART), F32),
            pltpu.VMEM((SETS, 1, units), F32),
            pltpu.VMEM((2, groups, 1, samples + EXTRA), F32),
            pltpu.VMEM((2, ranks, 1, samples + EXTRA), F32),
            pltpu.VMEM((3, SETS, 8, 128), F32),
            dma((4,)),
            dma((4,)),
            dma((parts, 5)),
            dma((parts, 5)),
            dma((parts, 5)),
            dma((parts, 5)),
            dma((parts, 3)),
            dma((parts, 3)),
            dma((2, groups)),
            dma((2, groups)),
            dma((2, ranks)),
            dma((2, ranks)),
            dma((3, SETS)),
            dma((3, SETS)),
            dma((SETS,)),
            dma((SETS,)),
        ],
        compiler_params=pltpu.CompilerParams(
            collective_id=0, has_side_effects=True, vmem_limit_bytes=62 * 1024 * 1024
        ),
    )(spins_packed, weight, hidden_bias.reshape(1, -1), force_w, force_b.reshape(1, -1))
    return update_w, update_b.reshape(-1)


def solution(mesh):
    placed = (P(None, "smp"), P(None, "grp"), P("grp"), P("smp", "grp"), P("grp"))
    return jax.shard_map(
        functools.partial(body, mesh.shape["grp"], mesh.shape["smp"]),
        mesh=mesh, in_specs=placed, out_specs=(P("smp", "grp"), P("grp")), check_vma=False,
    )
```

time: 221 us -> 101 us (0.46)
  Pallas kernels: 218 us -> 97.2 us
    pallas_call x1, Pallas kernels: 218 us -> 97.2 us  [body(): pl.pallas_call(functools.partial(kernel, groups, ranks), out_shape=(jax.S...]
where the time goes in v1:
time: 101 us
  Pallas kernels  97.2 us (96%)
  local copies, waits for them, and re-layouts  2.85 us (3%)
    pallas_call x1, Pallas kernels, body(): pl.pallas_call(functools.partial(kernel, groups, ranks), out_shape=(jax.S...  97.2 us
    unnamed x2, local copies, waits for them, and re-layouts  2.85 us

profile of v1, /device:TPU:1, one launch (start us, length us, event | category | flops | bytes accessed | tf_op | source)
XLA Modules:
  0.0 100.7 jit_solution(5577955894049863845)
XLA Ops:
  0.6 97.2 %shard_map.68 = (f32[32,1024]{1,0:T(8,128)}, f32[1,1024]{1,0:T(1,128)}) custom-call(s32[32,1024]{1,0:T(8,128)} %packed_ref.1, bf16[1024,1024]{1,0:T(8,128)(2,1)} %weight_ref.1, f32[1,1024]{1,0:T(1,128)} %bitcast.3, f32[32,1024]{1,0:T(8,128)} %force_ref.1, f32[1,1024]{1,0:T(1,128)} %bitcast.4), custom_call_target="tpu_custom_call" | custom-call | tf_op jit(solution)/shard_map/pallas_call | solution.py:424
  97.8 1.6 %copy.9 = f32[32,1024]{1,0:T(8,128)} copy(f32[32,1024]{1,0:T(8,128)} %get-tuple-element.8) | data formatting | bytes 262144
  99.4 1.3 %copy.10 = f32[1024]{0:T(1024)} copy(f32[1024]{0:T(1024)} %bitcast.5) | data formatting | bytes 8192

commit v2 on v1

v2 whole, which is shorter than its diff:
```python
import functools

import jax
import jax.numpy as jnp
from jax import lax
from jax.experimental import pallas as pl
from jax.experimental.pallas import tpu as pltpu
from jax.sharding import PartitionSpec as P

MESH = pl.DeviceIdType.MESH
F32, BF16 = jnp.float32, jnp.bfloat16
diag_shift = 0.01
SETS = 8
EXTRA = 256
PAD = 16
PART = 256
LINE = 4


def total(x):
    return jnp.sum(jnp.sum(x, axis=0, keepdims=True), axis=1, keepdims=True)


def kernel(
    groups, shards,
    packed_in, weight_in, bias_in, force_in, force_b_in,
    out_ref, out_b_ref,
    packed, weight, weight_t, bias_ref, bias_t, force_b_ref, tile, spins, hidden, force_all, lhs, scaled,
    image, image_core, image_z, image_x, image_all, image_b, by_group, by_rank, by_set, by_shard,
    load, spin_send, spin_recv, pass_send, pass_recv, force_send, force_recv, image_send, image_recv,
    group_send, group_recv, rank_send, rank_recv, set_send, set_recv, bias_send, bias_recv, shard_send, shard_recv,
):
    grp, smp = lax.axis_index("grp"), lax.axis_index("smp")
    words, here = packed_in.shape
    inputs, units = weight.shape
    rows = force_in.shape[0]
    ranks = shards // SETS
    pair = SETS * rows
    samples = ranks * here
    count = samples * SETS
    quarter = here // LINE
    parts = units // PART
    depth = 2 * ranks

    core, z, half = lax.rem(smp, 2), lax.rem(smp // 2, depth), smp // (2 * depth)
    parity, rank = lax.rem(z, 2), z // 2
    member = (core * 2 + parity) * 2 + half
    y, column = lax.rem(grp, LINE), grp // LINE

    def device(half_at, z_at, core_at):
        return {"smp": (half_at * depth + z_at) * 2 + core_at}

    sibling = device(half, z, 1 - core)
    z_partner = device(half, z + 1 - 2 * parity, core)
    x_partner = device(1 - half, z, core)

    def group_device(at):
        return {"grp": at}

    def line_device(at):
        return {"grp": column * LINE + at}

    def rank_device(at):
        return device(half, 2 * at + parity, core)

    def set_device(at):
        return device(lax.rem(at, 2), 2 * rank + lax.rem(at // 2, 2), at // 4)

    def shard_device(at):
        return {"smp": at}

    def remote(source, target, send, recv, where):
        return pltpu.make_async_remote_copy(
            source, target, send, recv, device_id=where, device_id_type=MESH
        )

    barrier = pltpu.get_barrier_semaphore()
    for size, me, peer in ((groups, grp, group_device), (ranks, rank, rank_device)):
        for step in range(1, size):
            pl.semaphore_signal(barrier, device_id=peer(lax.rem(me + step, size)), device_id_type=MESH)
    for where in (sibling, z_partner, x_partner):
        pl.semaphore_signal(barrier, device_id=where, device_id_type=MESH)

    def cols_of(at):
        return slice(at * PART, (at + 1) * PART)

    loads = [
        pltpu.make_async_copy(weight_in, weight, load.at[0]),
        pltpu.make_async_copy(bias_in, bias_ref, load.at[1]),
        pltpu.make_async_copy(force_b_in, force_b_ref, load.at[2]),
    ]
    for at in range(LINE):
        loads.append(
            pltpu.make_async_copy(packed_in.at[:, pl.ds(at * quarter, quarter)], packed.at[rank, at], load.at[3 + at])
        )
    for at in range(parts):
        loads.append(
            pltpu.make_async_copy(
                force_in.at[:, pl.ds(at * PART, PART)], force_all.at[at, core, parity, half], load.at[3 + LINE + at]
            )
        )
    for copy in loads:
        copy.start()
    for copy in loads:
        copy.wait()

    def turn(at, carry):
        cols = pl.ds(pl.multiple_of(at * 256, 256), 256)
        weight_t[cols, :] = weight[:, cols].T
        bias_t[cols, :] = jnp.broadcast_to(bias_ref[:, cols], (128, 256)).T
        return carry

    with jax.named_scope("turn"):
        lax.fori_loop(0, units // 256, turn, 0)
    with jax.named_scope("barrier"):
        pl.semaphore_wait(barrier, groups + ranks + 1)

    after, before, across = lax.rem(rank + 1, ranks), lax.rem(rank + ranks - 1, ranks), lax.rem(rank + 2, ranks)

    def force_send_own(at, which, where):
        own = force_all.at[at, core, parity, half]
        remote(own, own, force_send.at[at, which], force_recv.at[at, which], where).start()

    def force_arrived(at, which):
        target = (
            force_all.at[at, core, 1 - parity, half],
            force_all.at[at, core, parity, 1 - half],
            force_all.at[at, core, 1 - parity, 1 - half],
            force_all.at[at, 1 - core, parity],
            force_all.at[at, 1 - core, 1 - parity],
        )[which]
        remote(target, target, force_send.at[at, which], force_recv.at[at, which], sibling).wait_recv()

    def force_x(at):
        force_arrived(at, 1)
        block_x = force_all.at[at, core, parity, 1 - half]
        remote(block_x, block_x, force_send.at[at, 2], force_recv.at[at, 2], z_partner).start()
        ours = force_all.at[at, core, parity]
        remote(ours, ours, force_send.at[at, 3], force_recv.at[at, 3], sibling).start()

    def force_z(at):
        force_arrived(at, 0)
        force_arrived(at, 2)
        theirs = force_all.at[at, core, 1 - parity]
        remote(theirs, theirs, force_send.at[at, 4], force_recv.at[at, 4], sibling).start()

    def force_whole(at):
        force_arrived(at, 3)
        force_arrived(at, 4)

    def spin_send_to(step):
        own = packed.at[rank, y]
        return remote(own, own, spin_send.at[step], spin_recv.at[rank], rank_device(lax.rem(rank + step, ranks)))

    def spin_arrived(source):
        target = packed.at[source, y]
        remote(target, target, spin_send.at[0], spin_recv.at[source], sibling).wait_recv()

    def hand_on(source, slot):
        copies = []
        for step in range(1, LINE):
            piece = packed.at[source, y]
            copies.append(
                remote(
                    piece, piece, pass_send.at[slot, step], pass_recv.at[source, y],
                    line_device(lax.rem(y + step, LINE)),
                )
            )
            copies[-1].start()
        return copies

    def handed(source, step):
        from_y = lax.rem(y + step, LINE)
        target = packed.at[source, from_y]
        remote(target, target, pass_send.at[0, 0], pass_recv.at[source, from_y], sibling).wait_recv()
        return source, from_y

    for at in range(parts):
        force_send_own(at, 1, x_partner)
    spin_copies = [spin_send_to(step) for step in (1, ranks - 1, 2)]
    for copy in spin_copies:
        copy.start()
    for at in range(parts):
        force_send_own(at, 0, z_partner)

    masks = jnp.left_shift(1, lax.broadcasted_iota(jnp.int32, (32, quarter), 0))

    def hidden_pair(*pieces):
        cols = [pl.ds(pl.multiple_of(source * here + at * quarter, quarter), quarter) for source, at in pieces]
        for which, (source, at) in enumerate(pieces):
            to = slice(which * quarter, (which + 1) * quarter)
            for word in range(words):
                bits = jnp.bitwise_and(jnp.broadcast_to(packed[source, at, word : word + 1, :], (32, quarter)), masks)
                tile[word * 32 : word * 32 + 32, to] = jnp.where(bits != 0, 1.0, -1.0).astype(BF16)
        for to in range(SETS):
            word = (to % 2) * 2 * depth + 4 * rank + 2 * (to // 2 % 2) + to // 4
            from_rows = pl.ds(pl.multiple_of(word * rows, rows), rows)
            for which in range(2):
                spins[to * rows : (to + 1) * rows, cols[which]] = tile[
                    from_rows, which * quarter : (which + 1) * quarter
                ]
        for unit in range(0, units, 512):
            these = pl.ds(unit, 512)
            pre = jnp.dot(weight_t[these, :], tile[...], preferred_element_type=F32)
            pre = pre + jnp.concatenate([bias_t[these, :]] * (2 * quarter // 128), axis=1)
            result = jnp.tanh(pre).astype(BF16)
            for which in range(2):
                hidden[these, cols[which]] = result[:, which * quarter : (which + 1) * quarter]

    def own_pair(at, carry):
        hidden_pair((rank, 2 * at), (rank, 2 * at + 1))
        return carry

    with jax.named_scope("hidden0"):
        lax.fori_loop(0, LINE // 2, own_pair, 0)
    with jax.named_scope("spinab"):
        spin_arrived(before)
        passed = hand_on(before, 0)
        spin_arrived(after)
        passed += hand_on(after, 1)
    with jax.named_scope("hidden1"):
        hidden_pair((before, y), (after, y))
    with jax.named_scope("spinc"):
        spin_arrived(across)
        passed += hand_on(across, 2)
        piece = handed(before, 1)
    with jax.named_scope("hidden2"):
        hidden_pair((across, y), piece)

    def third(at, carry):
        first = jnp.where(at == 0, before, after)
        second = jnp.where(at == 0, after, before)
        with jax.named_scope("w3"):
            force_x(2 * at)
            force_x(2 * at + 1)
            pieces = handed(first, 3), handed(second, 1 + at)
        hidden_pair(*pieces)
        return carry

    def fourth(at, carry):
        first = jnp.where(at == 0, after, across)
        with jax.named_scope("w4"):
            pieces = handed(first, 2 + at), handed(across, 1 + at)
            force_z(2 * at)
            force_z(2 * at + 1)
        hidden_pair(*pieces)
        return carry

    with jax.named_scope("hidden3"):
        lax.fori_loop(0, 2, third, 0)
    with jax.named_scope("hidden4"):
        lax.fori_loop(0, 2, fourth, 0)

    wide_block = min(2048, samples)

    def values_part(which, at, slots, row):
        for to in range(SETS):
            lhs[to * rows : (to + 1) * rows, cols_of(at)] = slots[at, to // 4, to // 2 % 2, to % 2].astype(BF16)
        lhs[pair:, cols_of(at)] = jnp.concatenate(
            [row[:, cols_of(at)] / ranks, jnp.zeros((PAD - 1, PART), F32)], axis=0
        ).astype(BF16)

        def run(to, carry):
            cols = pl.ds(pl.multiple_of(to * wide_block, wide_block), wide_block)
            product = jnp.dot(lhs[:, cols_of(at)], hidden[cols_of(at), cols], preferred_element_type=F32)
            value = jnp.sum(product[:pair] * spins[:, cols].astype(F32), axis=0, keepdims=True) + product[pair : pair + 1]
            by_group[which, grp, :, cols] = value if at == 0 else by_group[which, grp, :, cols] + value
            return carry

        lax.fori_loop(0, samples // wide_block, run, 0)

    for at in range(parts):
        with jax.named_scope("forcew"):
            force_whole(at)
        with jax.named_scope("values0"):
            values_part(0, at, force_all, force_b_ref)

    def gather(slot, size, me, peer, send, recv):
        copies = []
        for step in range(1, size):
            copies.append(remote(slot(me), slot(me), send.at[step], recv.at[me], peer(lax.rem(me + step, size))))
            copies[-1].start()

        def finish():
            for step in range(1, size):
                source = lax.rem(me + size - step, size)
                remote(slot(source), slot(source), send.at[step], recv.at[source], sibling).wait_recv()
            for copy in copies:
                copy.wait_send()

        return finish

    def wide(x, lanes=128):
        return jnp.broadcast_to(x, (1, lanes))

    def sum_groups(which, first, second):
        by_group[which, grp, :, samples:] = jnp.concatenate([wide(first), wide(second)], axis=1)
        with jax.named_scope("redg"):
            gather(lambda at: by_group.at[which, at], groups, grp, group_device, group_send.at[which], group_recv.at[which])()
            mine = by_group[which, 0]
            for source in range(1, groups):
                mine = mine + by_group[which, source]
            by_rank[which, rank] = mine
        return mine, gather(
            lambda at: by_rank.at[which, at], ranks, rank, rank_device, rank_send.at[which], rank_recv.at[which]
        )

    def sum_ranks(which):
        whole = by_rank[which, 0]
        for source in range(1, ranks):
            whole = whole + by_rank[which, source]
        return whole[:, :samples], whole[:, samples : samples + 1], whole[:, samples + 128 : samples + 129]

    def gather_sets(which, values):
        fill = jnp.zeros((8 - len(values), 128), F32)
        by_set[which, member] = jnp.concatenate([wide(value) for value in values] + [fill], axis=0)
        return gather(lambda at: by_set.at[which, at], SETS, member, set_device, set_send.at[which], set_recv.at[which])

    def set_sum(which, row):
        value = by_set[which, 0, row : row + 1, :]
        for source in range(1, SETS):
            value = value + by_set[which, source, row : row + 1, :]
        return value[:, :1]

    def own_force(at):
        return force_all[at, core, parity, half]

    force_dot = total(force_b_ref[...] * force_b_ref[...]) / shards
    for at in range(parts):
        force_dot = force_dot + total(own_force(at) * own_force(at))
    mine, finish_ranks = sum_groups(0, force_dot, jnp.zeros((1, 1), F32))
    with jax.named_scope("redr"):
        by_shard[smp] = wide(total(mine[:, :samples]))
        finish_mean = gather(lambda at: by_shard.at[at], shards, smp, shard_device, shard_send, shard_recv)
        finish_ranks()
        values0, own_dot, _ = sum_ranks(0)
    with jax.named_scope("mean"):
        finish_mean()
        mean0 = by_shard[0]
        for source in range(1, shards):
            mean0 = mean0 + by_shard[source]
        centred = values0 - mean0[:, :1] / count
    with jax.named_scope("scaled"):
        for at in range(0, samples, 512):
            weights = centred[:, at : at + 512]
            scaled[:pair, at : at + 512] = (spins[:, at : at + 512].astype(F32) * weights).astype(BF16)
            scaled[pair:, at : at + 512] = jnp.concatenate(
                [weights, jnp.zeros((PAD - 1, 512), F32)], axis=0
            ).astype(BF16)

    def image_copy(at, which):
        source, target, where = (
            (image.at[at, 1 - core], image_core.at[at], sibling),
            (image.at[at, core, 1 - parity], image_z.at[at], z_partner),
            (image.at[at, core, parity], image_x.at[at], x_partner),
            (image_all.at[at, core, parity], image_all.at[at, core, parity], z_partner),
            (image_all.at[at, core, parity], image_all.at[at, core, parity], sibling),
            (image_all.at[at, core, 1 - parity], image_all.at[at, core, 1 - parity], sibling),
        )[which]
        return remote(source, target, image_send.at[at, which], image_recv.at[at, which], where)

    def image_arrived(at, which):
        target = (
            image_core.at[at], image_z.at[at], image_x.at[at],
            image_all.at[at, core, 1 - parity], image_all.at[at, 1 - core, parity], image_all.at[at, 1 - core, 1 - parity],
        )[which]
        remote(target, target, image_send.at[at, which], image_recv.at[at, which], sibling).wait_recv()

    def image_part(at):
        part = lax.dot_general(
            scaled[...], hidden[cols_of(at), :], (((1,), (1,)), ((), ())), preferred_element_type=F32
        )
        for to in range(SETS):
            image[at, to // 4, to // 2 % 2, to % 2] = part[to * rows : (to + 1) * rows]
        image_copy(at, 0).start()
        image_b[member, :, cols_of(at)] = part[pair : pair + 1]

    def sum_core(at):
        image_arrived(at, 0)
        image[at, core, 1 - parity] = image[at, core, 1 - parity] + image_core[at, 1 - parity]
        image_copy(at, 1).start()
        image[at, core, parity] = image[at, core, parity] + image_core[at, parity]

    def sum_z(at):
        image_arrived(at, 1)
        image[at, core, parity] = image[at, core, parity] + image_z[at]
        image_copy(at, 2).start()

    def sum_x(at):
        image_arrived(at, 2)
        image_all[at, core, parity] = image[at, core, parity] + image_x[at]
        image_copy(at, 3).start()
        image_copy(at, 4).start()

    def share_z(at):
        image_arrived(at, 3)
        image_copy(at, 5).start()

    def image_values(at):
        image_arrived(at, 4)
        image_arrived(at, 5)
        values_part(1, at, image_all, image_b[0])

    def named(name, step, *at):
        with jax.named_scope(name):
            step(*at)

    named("image", image_part, 0)
    finish_moment = gather_sets(0, [total(centred * centred), own_dot])
    named("image", image_part, 1)
    named("core", sum_core, 0)
    named("image", image_part, 2)
    named("core", sum_core, 1)
    named("image", image_part, 3)
    finish_bias = gather(lambda at: image_b.at[at], SETS, member, set_device, bias_send, bias_recv)
    named("core", sum_core, 2)
    named("core", sum_core, 3)
    named("sumz", sum_z, 0)
    named("sumz", sum_z, 1)
    with jax.named_scope("bias"):
        finish_moment()
        finish_bias()
        norm0 = set_sum(0, 1)
        step0 = norm0 / (set_sum(0, 0) / count + diag_shift * norm0)
        keep = 1.0 - diag_shift * step0
        pull = step0 / count
        whole_b = image_b[0]
        for source in range(1, SETS):
            whole_b = whole_b + image_b[source]
        image_b[0] = whole_b
    named("sumz", sum_z, 2)
    named("sumx", sum_x, 0)
    named("sumz", sum_z, 3)
    named("sumx", sum_x, 1)
    named("sumx", sum_x, 2)
    named("sharez", share_z, 0)
    named("sumx", sum_x, 3)
    named("values1", image_values, 0)
    named("sharez", share_z, 1)
    with jax.named_scope("norm"):
        residual_b = keep * force_b_ref[...] - pull * whole_b
        own_norm = total(residual_b * residual_b) / shards
        own_cross = total(residual_b * force_b_ref[...]) / shards
        for at in range(parts):
            residual = keep * own_force(at) - pull * image_all[at, core, parity, half]
            own_norm = own_norm + total(residual * residual)
            own_cross = own_cross + total(residual * own_force(at))
        finish_norm = gather_sets(1, [own_norm, own_cross])
    named("values1", image_values, 1)
    named("sharez", share_z, 2)
    named("values1", image_values, 2)
    named("sharez", share_z, 3)
    named("values1", image_values, 3)
    named("fnorm", finish_norm)

    _, finish_ranks = sum_groups(1, set_sum(1, 0), set_sum(1, 1))
    with jax.named_scope("redr"):
        finish_ranks()
        values1, norm1, cross = sum_ranks(1)
    beta = norm1 / norm0
    with jax.named_scope("sets"):
        values1 = (keep + beta) * centred - pull * values1
        mean1 = total(values1) / samples
        values1 = values1 - mean1
        gather_sets(2, [mean1, total(values1 * values1)])()
        middle = set_sum(2, 0) / SETS
        spread = jnp.zeros((1, 1), F32)
        for source in range(SETS):
            shift = by_set[2, source, 0:1, :1] - middle
            spread = spread + shift * shift
        variance1 = (set_sum(2, 1) + samples * spread) / count
    direction_dot = norm1 + 2.0 * beta * cross + beta * beta * norm0
    step1 = norm1 / (variance1 + diag_shift * direction_dot)

    for_force = step0 + step1 * (keep + beta)
    for_image = step1 * pull
    with jax.named_scope("out"):
        for at in range(parts):
            out_ref[:, cols_of(at)] = for_force * own_force(at) - for_image * image_all[at, core, parity, half]
        out_b_ref[...] = for_force * force_b_ref[...] - for_image * image_b[0]

        for copy in spin_copies + passed:
            copy.wait_send()
        for at in range(parts):
            for which in range(5):
                target = force_all.at[at, core, parity] if which > 2 else force_all.at[at, core, parity, half]
                remote(target, target, force_send.at[at, which], force_recv.at[at, which], sibling).wait_send()
            for which in range(6):
                image_copy(at, which).wait_send()


def body(groups, shards, spins_packed, weight, hidden_bias, force_w, force_b):
    words, here = spins_packed.shape
    inputs, units = weight.shape
    rows = force_w.shape[0]
    ranks = shards // SETS
    samples, pair = ranks * here, SETS * rows
    parts = units // PART
    quarter = here // LINE
    vmem = pl.BlockSpec(memory_space=pltpu.VMEM)
    anywhere = pl.BlockSpec(memory_space=pl.ANY)
    dma = pltpu.SemaphoreType.DMA
    update_w, update_b = pl.pallas_call(
        functools.partial(kernel, groups, shards),
        out_shape=(jax.ShapeDtypeStruct((rows, units), F32), jax.ShapeDtypeStruct((1, units), F32)),
        in_specs=[anywhere] * 5,
        out_specs=(vmem, vmem),
        scratch_shapes=[
            pltpu.VMEM((ranks, LINE, words, quarter), jnp.int32),
            pltpu.VMEM((inputs, units), BF16),
            pltpu.VMEM((units, inputs), BF16),
            pltpu.VMEM((1, units), F32),
            pltpu.VMEM((units, 128), F32),
            pltpu.VMEM((1, units), F32),
            pltpu.VMEM((inputs, 2 * quarter), BF16),
            pltpu.VMEM((pair, samples), BF16),
            pltpu.VMEM((units, samples), BF16),
            pltpu.VMEM((parts, 2, 2, 2, rows, PART), F32),
            pltpu.VMEM((pair + PAD, units), BF16),
            pltpu.VMEM((pair + PAD, samples), BF16),
            pltpu.VMEM((parts, 2, 2, 2, rows, PART), F32),
            pltpu.VMEM((parts, 2, 2, rows, PART), F32),
            pltpu.VMEM((parts, 2, rows, PART), F32),
            pltpu.VMEM((parts, 2, rows, PART), F32),
            pltpu.VMEM((parts, 2, 2, 2, rows, PART), F32),
            pltpu.VMEM((SETS, 1, units), F32),
            pltpu.VMEM((2, groups, 1, samples + EXTRA), F32),
            pltpu.VMEM((2, ranks, 1, samples + EXTRA), F32),
            pltpu.VMEM((3, SETS, 8, 128), F32),
            pltpu.VMEM((shards, 1, 128), F32),
            dma((3 + LINE + parts,)),
            dma((ranks,)),
            dma((ranks,)),
            dma((3, LINE)),
            dma((ranks, LINE)),
            dma((parts, 5)),
            dma((parts, 5)),
            dma((parts, 6)),
            dma((parts, 6)),
            dma((2, groups)),
            dma((2, groups)),
            dma((2, ranks)),
            dma((2, ranks)),
            dma((3, SETS)),
            dma((3, SETS)),
            dma((SETS,)),
            dma((SETS,)),
            dma((shards,)),
            dma((shards,)),
        ],
        compiler_params=pltpu.CompilerParams(
            collective_id=0, has_side_effects=True, vmem_limit_bytes=62 * 1024 * 1024
        ),
    )(spins_packed, weight, hidden_bias.reshape(1, -1), force_w, force_b.reshape(1, -1))
    return update_w, update_b.reshape(-1)


def solution(mesh):
    placed = (P(None, "smp"), P(None, "grp"), P("grp"), P("smp", "grp"), P("grp"))
    return jax.shard_map(
        functools.partial(body, mesh.shape["grp"], mesh.shape["smp"]),
        mesh=mesh, in_specs=placed, out_specs=(P("smp", "grp"), P("grp")), check_vma=False,
    )
```

time: 101 us -> 84.5 us (0.84)
  Pallas kernels: 97.2 us -> 80.9 us
    pallas_call x1, Pallas kernels: 97.2 us -> 80.9 us  [body(): pl.pallas_call(functools.partial(kernel, groups, shards), out_shape=(jax....]
where the time goes in v2:
time: 84.5 us; the launch traced here: 84.4 us
  Pallas kernels  80.9 us (96%)
  local copies, waits for them, and re-layouts  2.85 us (3%)
    pallas_call x1, Pallas kernels, body(): pl.pallas_call(functools.partial(kernel, groups, shards), out_shape=(jax....  80.9 us
    unnamed x2, local copies, waits for them, and re-layouts  2.85 us

profile of v2, /device:TPU:1, one launch (start us, length us, event | category | flops | bytes accessed | tf_op | source)
XLA Modules:
  0.0 84.4 jit_solution(6810220305641405081)
XLA Ops:
  0.6 80.9 %shard_map.68 = (f32[32,1024]{1,0:T(8,128)}, f32[1,1024]{1,0:T(1,128)}) custom-call(s32[32,1024]{1,0:T(8,128)} %packed_in.1, bf16[1024,1024]{1,0:T(8,128)(2,1)} %weight_in.1, f32[1,1024]{1,0:T(1,128)} %bitcast.3, f32[32,1024]{1,0:T(8,128)} %force_in.1, f32[1,1024]{1,0:T(1,128)} %bitcast.4), custom_call_target="tpu_custom_call" | custom-call | tf_op jit(solution)/shard_map/pallas_call | solution.py:503
  81.5 1.6 %copy.9 = f32[32,1024]{1,0:T(8,128)} copy(f32[32,1024]{1,0:T(8,128)} %get-tuple-element.8) | data formatting | bytes 262144
  83.1 1.3 %copy.10 = f32[1024]{0:T(1024)} copy(f32[1024]{0:T(1024)} %bitcast.5) | data formatting | bytes 8192

commit v3 on v2

--- a/solution.py
+++ b/solution.py
@@ -24,11 +24,11 @@
 def kernel(
     groups, shards,
     packed_in, weight_in, bias_in, force_in, force_b_in,
-    out_ref, out_b_ref,
+    image_ref, image_b_ref, own_ref, scale_ref,
     packed, weight, weight_t, bias_ref, bias_t, force_b_ref, tile, spins, hidden, force_all, lhs, scaled,
-    image, image_core, image_z, image_x, image_all, image_b, by_group, by_rank, by_set, by_shard,
+    image, image_core, image_z, image_x, image_all, image_b, by_group, by_rank, by_set, by_shard, by_total,
     load, spin_send, spin_recv, pass_send, pass_recv, force_send, force_recv, image_send, image_recv,
-    group_send, group_recv, rank_send, rank_recv, set_send, set_recv, bias_send, bias_recv, shard_send, shard_recv,
+    gather_send, gather_recv,
 ):
     grp, smp = lax.axis_index("grp"), lax.axis_index("smp")
     words, here = packed_in.shape
@@ -84,25 +84,32 @@
     def cols_of(at):
         return slice(at * PART, (at + 1) * PART)
 
-    loads = [
-        pltpu.make_async_copy(weight_in, weight, load.at[0]),
-        pltpu.make_async_copy(bias_in, bias_ref, load.at[1]),
-        pltpu.make_async_copy(force_b_in, force_b_ref, load.at[2]),
-    ]
-    for at in range(LINE):
-        loads.append(
-            pltpu.make_async_copy(packed_in.at[:, pl.ds(at * quarter, quarter)], packed.at[rank, at], load.at[3 + at])
-        )
-    for at in range(parts):
-        loads.append(
-            pltpu.make_async_copy(
-                force_in.at[:, pl.ds(at * PART, PART)], force_all.at[at, core, parity, half], load.at[3 + LINE + at]
+    def cols_ds(at):
+        return pl.ds(pl.multiple_of(at * PART, PART), PART)
+
+    def load_all():
+        copies = [
+            pltpu.make_async_copy(weight_in, weight, load.at[0]),
+            pltpu.make_async_copy(bias_in, bias_ref, load.at[1]),
+            pltpu.make_async_copy(force_b_in, force_b_ref, load.at[2]),
+        ]
+        for at in range(LINE):
+            copies.append(
+                pltpu.make_async_copy(packed_in.at[:, pl.ds(at * quarter, quarter)], packed.at[rank, at], load.at[3])
             )
-        )
-    for copy in loads:
-        copy.start()
-    for copy in loads:
-        copy.wait()
+        for at in range(parts):
+            copies.append(
+                pltpu.make_async_copy(force_in.at[:, cols_ds(at)], force_all.at[at, core, parity, half], load.at[4])
+            )
+        for copy in copies:
+            copy.start()
+        for copy in copies[:3]:
+            copy.wait()
+        pltpu.make_async_copy(packed.at[rank], packed.at[rank], load.at[3]).wait()
+        blocks = force_all.at[:, core, parity, half]
+        pltpu.make_async_copy(blocks, blocks, load.at[4]).wait()
+
+    load_all()
 
     def turn(at, carry):
         cols = pl.ds(pl.multiple_of(at * 256, 256), 256)
@@ -119,7 +126,7 @@
 
     def force_send_own(at, which, where):
         own = force_all.at[at, core, parity, half]
-        remote(own, own, force_send.at[at, which], force_recv.at[at, which], where).start()
+        remote(own, own, force_send.at[which], force_recv.at[at, which], where).start()
 
     def force_arrived(at, which):
         target = (
@@ -129,20 +136,20 @@
             force_all.at[at, 1 - core, parity],
             force_all.at[at, 1 - core, 1 - parity],
         )[which]
-        remote(target, target, force_send.at[at, which], force_recv.at[at, which], sibling).wait_recv()
+        remote(target, target, force_send.at[which], force_recv.at[at, which], sibling).wait_recv()
 
     def force_x(at):
         force_arrived(at, 1)
         block_x = force_all.at[at, core, parity, 1 - half]
-        remote(block_x, block_x, force_send.at[at, 2], force_recv.at[at, 2], z_partner).start()
+        remote(block_x, block_x, force_send.at[2], force_recv.at[at, 2], z_partner).start()
         ours = force_all.at[at, core, parity]
-        remote(ours, ours, force_send.at[at, 3], force_recv.at[at, 3], sibling).start()
+        remote(ours, ours, force_send.at[3], force_recv.at[at, 3], sibling).start()
 
     def force_z(at):
         force_arrived(at, 0)
         force_arrived(at, 2)
         theirs = force_all.at[at, core, 1 - parity]
-        remote(theirs, theirs, force_send.at[at, 4], force_recv.at[at, 4], sibling).start()
+        remote(theirs, theirs, force_send.at[4], force_recv.at[at, 4], sibling).start()
 
     def force_whole(at):
         force_arrived(at, 3)
@@ -150,36 +157,29 @@
 
     def spin_send_to(step):
         own = packed.at[rank, y]
-        return remote(own, own, spin_send.at[step], spin_recv.at[rank], rank_device(lax.rem(rank + step, ranks)))
+        return remote(own, own, spin_send.at[0], spin_recv.at[rank], rank_device(lax.rem(rank + step, ranks)))
 
     def spin_arrived(source):
         target = packed.at[source, y]
         remote(target, target, spin_send.at[0], spin_recv.at[source], sibling).wait_recv()
 
     def hand_on(source, slot):
-        copies = []
         for step in range(1, LINE):
             piece = packed.at[source, y]
-            copies.append(
-                remote(
-                    piece, piece, pass_send.at[slot, step], pass_recv.at[source, y],
-                    line_device(lax.rem(y + step, LINE)),
-                )
-            )
-            copies[-1].start()
-        return copies
+            remote(
+                piece, piece, pass_send.at[slot], pass_recv.at[source, y], line_device(lax.rem(y + step, LINE))
+            ).start()
 
     def handed(source, step):
         from_y = lax.rem(y + step, LINE)
         target = packed.at[source, from_y]
-        remote(target, target, pass_send.at[0, 0], pass_recv.at[source, from_y], sibling).wait_recv()
+        remote(target, target, pass_send.at[0], pass_recv.at[source, from_y], sibling).wait_recv()
         return source, from_y
 
     for at in range(parts):
         force_send_own(at, 1, x_partner)
-    spin_copies = [spin_send_to(step) for step in (1, ranks - 1, 2)]
-    for copy in spin_copies:
-        copy.start()
+    for step in (1, ranks - 1, 2):
+        spin_send_to(step).start()
     for at in range(parts):
         force_send_own(at, 0, z_partner)
 
@@ -215,14 +215,14 @@
         lax.fori_loop(0, LINE // 2, own_pair, 0)
     with jax.named_scope("spinab"):
         spin_arrived(before)
-        passed = hand_on(before, 0)
+        hand_on(before, 0)
         spin_arrived(after)
-        passed += hand_on(after, 1)
+        hand_on(after, 1)
     with jax.named_scope("hidden1"):
         hidden_pair((before, y), (after, y))
     with jax.named_scope("spinc"):
         spin_arrived(across)
-        passed += hand_on(across, 2)
+        hand_on(across, 2)
         piece = handed(before, 1)
     with jax.named_scope("hidden2"):
         hidden_pair((across, y), piece)
@@ -253,57 +253,57 @@
 
     wide_block = min(2048, samples)
 
-    def values_part(which, at, slots, row):
+    def fill_lhs(at, slots, row):
         for to in range(SETS):
             lhs[to * rows : (to + 1) * rows, cols_of(at)] = slots[at, to // 4, to // 2 % 2, to % 2].astype(BF16)
         lhs[pair:, cols_of(at)] = jnp.concatenate(
             [row[:, cols_of(at)] / ranks, jnp.zeros((PAD - 1, PART), F32)], axis=0
         ).astype(BF16)
 
+    def values_of(which, first, last):
+        these = slice(first * PART, last * PART)
+
         def run(to, carry):
             cols = pl.ds(pl.multiple_of(to * wide_block, wide_block), wide_block)
-            product = jnp.dot(lhs[:, cols_of(at)], hidden[cols_of(at), cols], preferred_element_type=F32)
+            product = jnp.dot(lhs[:, these], hidden[these, cols], preferred_element_type=F32)
             value = jnp.sum(product[:pair] * spins[:, cols].astype(F32), axis=0, keepdims=True) + product[pair : pair + 1]
-            by_group[which, grp, :, cols] = value if at == 0 else by_group[which, grp, :, cols] + value
+            by_group[which, grp, :, cols] = value if first == 0 else by_group[which, grp, :, cols] + value
             return carry
 
         lax.fori_loop(0, samples // wide_block, run, 0)
 
-    for at in range(parts):
-        with jax.named_scope("forcew"):
+    with jax.named_scope("forcew"):
+        for at in range(parts):
             force_whole(at)
-        with jax.named_scope("values0"):
-            values_part(0, at, force_all, force_b_ref)
-
-    def gather(slot, size, me, peer, send, recv):
-        copies = []
+            fill_lhs(at, force_all, force_b_ref)
+    with jax.named_scope("values0"):
+        values_of(0, 0, parts)
+
+    def gather(slots, which, size, me, peer):
+        send, recv = gather_send.at[which], gather_recv.at[which]
         for step in range(1, size):
-            copies.append(remote(slot(me), slot(me), send.at[step], recv.at[me], peer(lax.rem(me + step, size))))
-            copies[-1].start()
+            remote(slots.at[me], slots.at[me], send, recv, peer(lax.rem(me + step, size))).start()
+        others = slots.at[pl.ds(0, size - 1)]
 
         def finish():
-            for step in range(1, size):
-                source = lax.rem(me + size - step, size)
-                remote(slot(source), slot(source), send.at[step], recv.at[source], sibling).wait_recv()
-            for copy in copies:
-                copy.wait_send()
+            remote(others, others, send, recv, sibling).wait()
 
         return finish
 
     def wide(x, lanes=128):
         return jnp.broadcast_to(x, (1, lanes))
 
-    def sum_groups(which, first, second):
+    def sum_groups(which, first, second, between):
         by_group[which, grp, :, samples:] = jnp.concatenate([wide(first), wide(second)], axis=1)
         with jax.named_scope("redg"):
-            gather(lambda at: by_group.at[which, at], groups, grp, group_device, group_send.at[which], group_recv.at[which])()
+            finish = gather(by_group.at[which], which, groups, grp, group_device)
+            between()
+            finish()
             mine = by_group[which, 0]
             for source in range(1, groups):
                 mine = mine + by_group[which, source]
             by_rank[which, rank] = mine
-        return mine, gather(
-            lambda at: by_rank.at[which, at], ranks, rank, rank_device, rank_send.at[which], rank_recv.at[which]
-        )
+        return gather(by_rank.at[which], 2 + which, ranks, rank, rank_device)
 
     def sum_ranks(which):
         whole = by_rank[which, 0]
@@ -314,7 +314,7 @@
     def gather_sets(which, values):
         fill = jnp.zeros((8 - len(values), 128), F32)
         by_set[which, member] = jnp.concatenate([wide(value) for value in values] + [fill], axis=0)
-        return gather(lambda at: by_set.at[which, at], SETS, member, set_device, set_send.at[which], set_recv.at[which])
+        return gather(by_set.at[which], 4 + which, SETS, member, set_device)
 
     def set_sum(which, row):
         value = by_set[which, 0, row : row + 1, :]
@@ -328,17 +328,28 @@
     force_dot = total(force_b_ref[...] * force_b_ref[...]) / shards
     for at in range(parts):
         force_dot = force_dot + total(own_force(at) * own_force(at))
-    mine, finish_ranks = sum_groups(0, force_dot, jnp.zeros((1, 1), F32))
+    by_shard[smp] = wide(total(by_group[0, grp, :, :samples]))
+    finish_shards = []
+
+    def total_shards():
+        finish_shards.append(gather(by_shard, 8, shards, smp, shard_device))
+
+    finish_ranks = sum_groups(0, force_dot, jnp.zeros((1, 1), F32), total_shards)
+    with jax.named_scope("shards"):
+        finish_shards[0]()
+        mine = by_shard[0]
+        for source in range(1, shards):
+            mine = mine + by_shard[source]
+        by_total[grp] = mine
+        finish_total = gather(by_total, 9, groups, grp, group_device)
     with jax.named_scope("redr"):
-        by_shard[smp] = wide(total(mine[:, :samples]))
-        finish_mean = gather(lambda at: by_shard.at[at], shards, smp, shard_device, shard_send, shard_recv)
         finish_ranks()
         values0, own_dot, _ = sum_ranks(0)
     with jax.named_scope("mean"):
-        finish_mean()
-        mean0 = by_shard[0]
-        for source in range(1, shards):
-            mean0 = mean0 + by_shard[source]
+        finish_total()
+        mean0 = by_total[0]
+        for source in range(1, groups):
+            mean0 = mean0 + by_total[source]
         centred = values0 - mean0[:, :1] / count
     with jax.named_scope("scaled"):
         for at in range(0, samples, 512):
@@ -357,23 +368,23 @@
             (image_all.at[at, core, parity], image_all.at[at, core, parity], sibling),
             (image_all.at[at, core, 1 - parity], image_all.at[at, core, 1 - parity], sibling),
         )[which]
-        return remote(source, target, image_send.at[at, which], image_recv.at[at, which], where)
+        return remote(source, target, image_send.at[which], image_recv.at[at, which], where)
 
     def image_arrived(at, which):
         target = (
             image_core.at[at], image_z.at[at], image_x.at[at],
             image_all.at[at, core, 1 - parity], image_all.at[at, 1 - core, parity], image_all.at[at, 1 - core, 1 - parity],
         )[which]
-        remote(target, target, image_send.at[at, which], image_recv.at[at, which], sibling).wait_recv()
+        remote(target, target, image_send.at[which], image_recv.at[at, which], sibling).wait_recv()
 
     def image_part(at):
         part = lax.dot_general(
-            scaled[...], hidden[cols_of(at), :], (((1,), (1,)), ((), ())), preferred_element_type=F32
+            scaled[...], hidden[cols_ds(at), :], (((1,), (1,)), ((), ())), preferred_element_type=F32
         )
         for to in range(SETS):
             image[at, to // 4, to // 2 % 2, to % 2] = part[to * rows : (to + 1) * rows]
         image_copy(at, 0).start()
-        image_b[member, :, cols_of(at)] = part[pair : pair + 1]
+        image_b[member, :, cols_ds(at)] = part[pair : pair + 1]
 
     def sum_core(at):
         image_arrived(at, 0)
@@ -399,24 +410,34 @@
     def image_values(at):
         image_arrived(at, 4)
         image_arrived(at, 5)
-        values_part(1, at, image_all, image_b[0])
+        fill_lhs(at, image_all, image_b[0])
+        values_of(1, at, at + 1)
 
     def named(name, step, *at):
         with jax.named_scope(name):
             step(*at)
 
-    named("image", image_part, 0)
     finish_moment = gather_sets(0, [total(centred * centred), own_dot])
-    named("image", image_part, 1)
-    named("core", sum_core, 0)
-    named("image", image_part, 2)
-    named("core", sum_core, 1)
-    named("image", image_part, 3)
-    finish_bias = gather(lambda at: image_b.at[at], SETS, member, set_device, bias_send, bias_recv)
-    named("core", sum_core, 2)
+
+    def image_step(at, carry):
+        image_part(at)
+
+        @pl.when(at > 0)
+        def _():
+            sum_core(at - 1)
+
+        return carry
+
+    with jax.named_scope("image"):
+        lax.fori_loop(0, parts, image_step, 0)
+    finish_bias = gather(image_b, 7, SETS, member, set_device)
     named("core", sum_core, 3)
     named("sumz", sum_z, 0)
     named("sumz", sum_z, 1)
+    named("sumz", sum_z, 2)
+    named("sumx", sum_x, 0)
+    named("sumz", sum_z, 3)
+    named("sumx", sum_x, 1)
     with jax.named_scope("bias"):
         finish_moment()
         finish_bias()
@@ -428,23 +449,24 @@
         for source in range(1, SETS):
             whole_b = whole_b + image_b[source]
         image_b[0] = whole_b
-    named("sumz", sum_z, 2)
-    named("sumx", sum_x, 0)
-    named("sumz", sum_z, 3)
-    named("sumx", sum_x, 1)
     named("sumx", sum_x, 2)
     named("sharez", share_z, 0)
+    named("values1", image_values, 0)
     named("sumx", sum_x, 3)
-    named("values1", image_values, 0)
     named("sharez", share_z, 1)
     with jax.named_scope("norm"):
         residual_b = keep * force_b_ref[...] - pull * whole_b
         own_norm = total(residual_b * residual_b) / shards
         own_cross = total(residual_b * force_b_ref[...]) / shards
+        image_b_ref[0:1, :] = whole_b
+        image_b_ref[1:2, :] = force_b_ref[...]
         for at in range(parts):
-            residual = keep * own_force(at) - pull * image_all[at, core, parity, half]
+            force, own = own_force(at), image_all[at, core, parity, half]
+            residual = keep * force - pull * own
             own_norm = own_norm + total(residual * residual)
-            own_cross = own_cross + total(residual * own_force(at))
+            own_cross = own_cross + total(residual * force)
+            image_ref[:, cols_of(at)] = own
+            own_ref[:, cols_of(at)] = force
         finish_norm = gather_sets(1, [own_norm, own_cross])
     named("values1", image_values, 1)
     named("sharez", share_z, 2)
@@ -453,7 +475,7 @@
     named("values1", image_values, 3)
     named("fnorm", finish_norm)
 
-    _, finish_ranks = sum_groups(1, set_sum(1, 0), set_sum(1, 1))
+    finish_ranks = sum_groups(1, set_sum(1, 0), set_sum(1, 1), lambda: None)
     with jax.named_scope("redr"):
         finish_ranks()
         values1, norm1, cross = sum_ranks(1)
@@ -474,19 +496,24 @@
 
     for_force = step0 + step1 * (keep + beta)
     for_image = step1 * pull
+    scale_ref[...] = jnp.concatenate([wide(for_force), wide(for_image), jnp.zeros((6, 128), F32)], axis=0)
     with jax.named_scope("out"):
-        for at in range(parts):
-            out_ref[:, cols_of(at)] = for_force * own_force(at) - for_image * image_all[at, core, parity, half]
-        out_b_ref[...] = for_force * force_b_ref[...] - for_image * image_b[0]
-
-        for copy in spin_copies + passed:
-            copy.wait_send()
-        for at in range(parts):
-            for which in range(5):
-                target = force_all.at[at, core, parity] if which > 2 else force_all.at[at, core, parity, half]
-                remote(target, target, force_send.at[at, which], force_recv.at[at, which], sibling).wait_send()
-            for which in range(6):
-                image_copy(at, which).wait_send()
+        pieces = packed.at[rank, pl.ds(0, LINE - 1)]
+        remote(pieces, pieces, spin_send.at[0], spin_recv.at[0], sibling).wait_send()
+        for slot in range(3):
+            remote(pieces, pieces, pass_send.at[slot], spin_recv.at[0], sibling).wait_send()
+        for which in range(5):
+            blocks = force_all.at[:, core, parity] if which > 2 else force_all.at[:, core, parity, half]
+            remote(blocks, blocks, force_send.at[which], spin_recv.at[0], sibling).wait_send()
+        for which in range(6):
+            blocks = image_core if which == 0 else image_z
+            remote(blocks, blocks, image_send.at[which], spin_recv.at[0], sibling).wait_send()
+
+
+def finish_kernel(image_ref, image_b_ref, force_ref, scale_ref, out_ref, out_b_ref):
+    for_force, for_image = scale_ref[0:1, 0:1], scale_ref[1:2, 0:1]
+    out_ref[...] = for_force * force_ref[...] - for_image * image_ref[...]
+    out_b_ref[...] = for_force * image_b_ref[1:2, :] - for_image * image_b_ref[0:1, :]
 
 
 def body(groups, shards, spins_packed, weight, hidden_bias, force_w, force_b):
@@ -500,11 +527,14 @@
     vmem = pl.BlockSpec(memory_space=pltpu.VMEM)
     anywhere = pl.BlockSpec(memory_space=pl.ANY)
     dma = pltpu.SemaphoreType.DMA
-    update_w, update_b = pl.pallas_call(
+    results = pl.pallas_call(
         functools.partial(kernel, groups, shards),
-        out_shape=(jax.ShapeDtypeStruct((rows, units), F32), jax.ShapeDtypeStruct((1, units), F32)),
+        out_shape=(
+            pltpu.VMEM((rows, units), F32), pltpu.VMEM((8, units), F32),
+            pltpu.VMEM((rows, units), F32), pltpu.VMEM((8, 128), F32),
+        ),
         in_specs=[anywhere] * 5,
-        out_specs=(vmem, vmem),
+        out_specs=(vmem,) * 4,
         scratch_shapes=[
             pltpu.VMEM((ranks, LINE, words, quarter), jnp.int32),
             pltpu.VMEM((inputs, units), BF16),
@@ -528,30 +558,29 @@
             pltpu.VMEM((2, ranks, 1, samples + EXTRA), F32),
             pltpu.VMEM((3, SETS, 8, 128), F32),
             pltpu.VMEM((shards, 1, 128), F32),
-            dma((3 + LINE + parts,)),
+            pltpu.VMEM((groups, 1, 128), F32),
+            dma((5,)),
+            dma((1,)),
             dma((ranks,)),
-            dma((ranks,)),
-            dma((3, LINE)),
+            dma((3,)),
             dma((ranks, LINE)),
+            dma((5,)),
             dma((parts, 5)),
-            dma((parts, 5)),
+            dma((6,)),
             dma((parts, 6)),
-            dma((parts, 6)),
-            dma((2, groups)),
-            dma((2, groups)),
-            dma((2, ranks)),
-            dma((2, ranks)),
-            dma((3, SETS)),
-            dma((3, SETS)),
-            dma((SETS,)),
-            dma((SETS,)),
-            dma((shards,)),
-            dma((shards,)),
+            dma((10,)),
+            dma((10,)),
         ],
         compiler_params=pltpu.CompilerParams(
             collective_id=0, has_side_effects=True, vmem_limit_bytes=62 * 1024 * 1024
         ),
     )(spins_packed, weight, hidden_bias.reshape(1, -1), force_w, force_b.reshape(1, -1))
+    update_w, update_b = pl.pallas_call(
+        finish_kernel,
+        out_shape=(jax.ShapeDtypeStruct((rows, units), F32), jax.ShapeDtypeStruct((1, units), F32)),
+        in_specs=[vmem] * 4,
+        out_specs=(vmem, vmem),
+    )(*[pltpu.with_memory_space_constraint(result, pltpu.VMEM) for result in results])
     return update_w, update_b.reshape(-1)
 
 

time: 84.5 us -> 77.8 us (0.921)
  Pallas kernels: 80.9 us -> 77.1 us
  local copies, waits for them, and re-layouts: 2.85 us -> 0 us
    pallas_call x1 -> x2, Pallas kernels: 80.9 us -> 77.1 us  [the longest x1 76.4 us: body(): pl.pallas_call(functools.partial(kernel, groups, shards), out_shape=(pltp...]
    unnamed x2 -> x0, local copies, waits for them, and re-layouts: 2.85 us -> none
where the time goes in v3:
time: 77.8 us; the launch traced here: 77.7 us
  Pallas kernels  77.1 us (99%)
    pallas_call x1, Pallas kernels, body(): pl.pallas_call(functools.partial(kernel, groups, shards), out_shape=(pltp...  76.4 us

profile of v3, /device:TPU:1, one launch (start us, length us, event | category | flops | bytes accessed | tf_op | source)
XLA Modules:
  0.0 77.7 jit_solution(5138392589035307105)
XLA Ops:
  0.6 76.4 %shard_map.68 = (f32[32,1024]{1,0:T(8,128)S(1)}, f32[8,1024]{1,0:T(8,128)S(1)}, f32[32,1024]{1,0:T(8,128)S(1)}, f32[8,128]{1,0:T(8,128)S(1)}) custom-call(s32[32,1024]{1,0:T(8,128)} %packed_in.1, bf16[1024,1024]{1,0:T(8,128)(2,1)} %weight_in.1, f32[1,1024]{1,0:T(1,128)} %bitcast.3, f32[32,1024]{1,0:T(8,128)} %force_in.1, f32[1,1024]{1,0:T(1,128)} %bitcast.4), custom_call_target="tpu_custom_call" | custom-call | tf_op jit(solution)/shard_map/pallas_call | solution.py:530
  77.0 0.7 shard_map.69

commit v4 on v3

--- a/solution.py
+++ b/solution.py
@@ -25,8 +25,8 @@
     groups, shards,
     packed_in, weight_in, bias_in, force_in, force_b_in,
     image_ref, image_b_ref, own_ref, scale_ref,
-    packed, weight, weight_t, bias_ref, bias_t, force_b_ref, tile, spins, hidden, force_all, lhs, scaled,
-    image, image_core, image_z, image_x, image_all, image_b, by_group, by_rank, by_set, by_shard, by_total,
+    packed, weight, weight_t, bias_ref, bias_t, force_b_ref, tile_a, tile_b, spins, hidden, force_all, lhs, scaled,
+    image, image_core, image_z, image_x, image_all, image_b, by_group_a, by_group_b, by_rank_a, by_rank_b, by_set, by_shard, by_total,
     load, spin_send, spin_recv, pass_send, pass_recv, force_send, force_recv, image_send, image_recv,
     gather_send, gather_recv,
 ):
@@ -119,9 +119,6 @@
 
     with jax.named_scope("turn"):
         lax.fori_loop(0, units // 256, turn, 0)
-    with jax.named_scope("barrier"):
-        pl.semaphore_wait(barrier, groups + ranks + 1)
-
     after, before, across = lax.rem(rank + 1, ranks), lax.rem(rank + ranks - 1, ranks), lax.rem(rank + 2, ranks)
 
     def force_send_own(at, which, where):
@@ -176,17 +173,13 @@
         remote(target, target, pass_send.at[0], pass_recv.at[source, from_y], sibling).wait_recv()
         return source, from_y
 
-    for at in range(parts):
-        force_send_own(at, 1, x_partner)
-    for step in (1, ranks - 1, 2):
-        spin_send_to(step).start()
-    for at in range(parts):
-        force_send_own(at, 0, z_partner)
-
     masks = jnp.left_shift(1, lax.broadcasted_iota(jnp.int32, (32, quarter), 0))
 
-    def hidden_pair(*pieces):
-        cols = [pl.ds(pl.multiple_of(source * here + at * quarter, quarter), quarter) for source, at in pieces]
+    def places(pieces):
+        return [pl.ds(pl.multiple_of(source * here + at * quarter, quarter), quarter) for source, at in pieces]
+
+    def unpack(tile, pieces):
+        cols = places(pieces)
         for which, (source, at) in enumerate(pieces):
             to = slice(which * quarter, (which + 1) * quarter)
             for word in range(words):
@@ -199,6 +192,9 @@
                 spins[to * rows : (to + 1) * rows, cols[which]] = tile[
                     from_rows, which * quarter : (which + 1) * quarter
                 ]
+
+    def activate(tile, pieces):
+        cols = places(pieces)
         for unit in range(0, units, 512):
             these = pl.ds(unit, 512)
             pre = jnp.dot(weight_t[these, :], tile[...], preferred_element_type=F32)
@@ -207,51 +203,58 @@
             for which in range(2):
                 hidden[these, cols[which]] = result[:, which * quarter : (which + 1) * quarter]
 
-    def own_pair(at, carry):
-        hidden_pair((rank, 2 * at), (rank, 2 * at + 1))
-        return carry
+    first, second = ((rank, 0), (rank, 1)), ((rank, 2), (rank, 3))
+    with jax.named_scope("unpack0"):
+        unpack(tile_a, first)
+    with jax.named_scope("barrier"):
+        pl.semaphore_wait(barrier, groups + ranks + 1)
+    for at in range(parts):
+        force_send_own(at, 1, x_partner)
+    for step in (1, ranks - 1, 2):
+        spin_send_to(step).start()
+    for at in range(parts):
+        force_send_own(at, 0, z_partner)
 
     with jax.named_scope("hidden0"):
-        lax.fori_loop(0, LINE // 2, own_pair, 0)
+        unpack(tile_b, second)
+        activate(tile_a, first)
+    with jax.named_scope("hidden1"):
+        activate(tile_b, second)
     with jax.named_scope("spinab"):
         spin_arrived(before)
         hand_on(before, 0)
         spin_arrived(after)
         hand_on(after, 1)
-    with jax.named_scope("hidden1"):
-        hidden_pair((before, y), (after, y))
+    with jax.named_scope("hidden2"):
+        pieces = ((before, y), (after, y))
+        unpack(tile_a, pieces)
+        activate(tile_a, pieces)
     with jax.named_scope("spinc"):
         spin_arrived(across)
         hand_on(across, 2)
-        piece = handed(before, 1)
-    with jax.named_scope("hidden2"):
-        hidden_pair((across, y), piece)
-
-    def third(at, carry):
-        first = jnp.where(at == 0, before, after)
-        second = jnp.where(at == 0, after, before)
-        with jax.named_scope("w3"):
-            force_x(2 * at)
-            force_x(2 * at + 1)
-            pieces = handed(first, 3), handed(second, 1 + at)
-        hidden_pair(*pieces)
-        return carry
-
-    def fourth(at, carry):
-        first = jnp.where(at == 0, after, across)
-        with jax.named_scope("w4"):
-            pieces = handed(first, 2 + at), handed(across, 1 + at)
-            force_z(2 * at)
-            force_z(2 * at + 1)
-        hidden_pair(*pieces)
-        return carry
-
-    with jax.named_scope("hidden3"):
-        lax.fori_loop(0, 2, third, 0)
+        for at in range(parts):
+            force_x(at)
+        pieces = ((across, y), handed(before, 1))
+    with jax.named_scope("unpack3"):
+        unpack(tile_b, pieces)
+    now, later = tile_b, tile_a
+    for step, ((source_a, from_a), (source_b, from_b)) in enumerate(
+        (((before, 3), (after, 1)), ((after, 3), (before, 2)), ((after, 2), (across, 1)), ((across, 3), (across, 2)))
+    ):
+        with jax.named_scope("wait"):
+            if step >= 2:
+                force_z(2 * step - 4)
+                force_z(2 * step - 3)
+            coming = (handed(source_a, from_a), handed(source_b, from_b))
+        with jax.named_scope("hidden3"):
+            unpack(later, coming)
+            activate(now, pieces)
+        now, later, pieces = later, now, coming
     with jax.named_scope("hidden4"):
-        lax.fori_loop(0, 2, fourth, 0)
-
-    wide_block = min(2048, samples)
+        activate(now, pieces)
+
+    span = samples // 2
+    by_group, by_rank = (by_group_a, by_group_b), (by_rank_a, by_rank_b)
 
     def fill_lhs(at, slots, row):
         for to in range(SETS):
@@ -260,25 +263,17 @@
             [row[:, cols_of(at)] / ranks, jnp.zeros((PAD - 1, PART), F32)], axis=0
         ).astype(BF16)
 
-    def values_of(which, first, last):
-        these = slice(first * PART, last * PART)
-
-        def run(to, carry):
-            cols = pl.ds(pl.multiple_of(to * wide_block, wide_block), wide_block)
-            product = jnp.dot(lhs[:, these], hidden[these, cols], preferred_element_type=F32)
-            value = jnp.sum(product[:pair] * spins[:, cols].astype(F32), axis=0, keepdims=True) + product[pair : pair + 1]
-            by_group[which, grp, :, cols] = value if first == 0 else by_group[which, grp, :, cols] + value
-            return carry
-
-        lax.fori_loop(0, samples // wide_block, run, 0)
+    def values_of(which, first, last, side):
+        these, cols = slice(first * PART, last * PART), slice(side * span, (side + 1) * span)
+        product = jnp.dot(lhs[:, these], hidden[these, cols], preferred_element_type=F32)
+        value = jnp.sum(product[:pair] * spins[:, cols].astype(F32), axis=0, keepdims=True) + product[pair : pair + 1]
+        mine = by_group[side].at[which, grp, :, :span]
+        mine[...] = value if first == 0 else mine[...] + value
 
     with jax.named_scope("forcew"):
         for at in range(parts):
             force_whole(at)
             fill_lhs(at, force_all, force_b_ref)
-    with jax.named_scope("values0"):
-        values_of(0, 0, parts)
-
     def gather(slots, which, size, me, peer):
         send, recv = gather_send.at[which], gather_recv.at[which]
         for step in range(1, size):
@@ -293,28 +288,26 @@
     def wide(x, lanes=128):
         return jnp.broadcast_to(x, (1, lanes))
 
-    def sum_groups(which, first, second, between):
-        by_group[which, grp, :, samples:] = jnp.concatenate([wide(first), wide(second)], axis=1)
-        with jax.named_scope("redg"):
-            finish = gather(by_group.at[which], which, groups, grp, group_device)
-            between()
-            finish()
-            mine = by_group[which, 0]
-            for source in range(1, groups):
-                mine = mine + by_group[which, source]
-            by_rank[which, rank] = mine
-        return gather(by_rank.at[which], 2 + which, ranks, rank, rank_device)
-
-    def sum_ranks(which):
-        whole = by_rank[which, 0]
+    def send_groups(which, side):
+        return gather(by_group[side].at[which], 2 * which + side, groups, grp, group_device)
+
+    def send_ranks(which, side):
+        mine = by_group[side][which, 0]
+        for source in range(1, groups):
+            mine = mine + by_group[side][which, source]
+        by_rank[side][which, rank] = mine
+        return gather(by_rank[side].at[which], 4 + 2 * which + side, ranks, rank, rank_device)
+
+    def sum_ranks(which, side):
+        whole = by_rank[side][which, 0]
         for source in range(1, ranks):
-            whole = whole + by_rank[which, source]
-        return whole[:, :samples], whole[:, samples : samples + 1], whole[:, samples + 128 : samples + 129]
+            whole = whole + by_rank[side][which, source]
+        return whole
 
     def gather_sets(which, values):
         fill = jnp.zeros((8 - len(values), 128), F32)
         by_set[which, member] = jnp.concatenate([wide(value) for value in values] + [fill], axis=0)
-        return gather(by_set.at[which], 4 + which, SETS, member, set_device)
+        return gather(by_set.at[which], 8 + which, SETS, member, set_device)
 
     def set_sum(which, row):
         value = by_set[which, 0, row : row + 1, :]
@@ -328,32 +321,47 @@
     force_dot = total(force_b_ref[...] * force_b_ref[...]) / shards
     for at in range(parts):
         force_dot = force_dot + total(own_force(at) * own_force(at))
-    by_shard[smp] = wide(total(by_group[0, grp, :, :samples]))
-    finish_shards = []
-
-    def total_shards():
-        finish_shards.append(gather(by_shard, 8, shards, smp, shard_device))
-
-    finish_ranks = sum_groups(0, force_dot, jnp.zeros((1, 1), F32), total_shards)
+    def extras(which, first, second):
+        by_group[1][which, grp, :, span:] = jnp.concatenate([wide(first), wide(second)], axis=1)
+
+    def own_sum(side):
+        return total(by_group[side][0, grp, :, :span])
+
+    with jax.named_scope("values0"):
+        values_of(0, 0, parts, 0)
+        finish_a = send_groups(0, 0)
+        extras(0, force_dot, jnp.zeros((1, 1), F32))
+        values_of(0, 0, parts, 1)
+        finish_b = send_groups(0, 1)
+    with jax.named_scope("redg"):
+        by_shard[smp] = wide(own_sum(0) + own_sum(1))
+        finish_shards = gather(by_shard, 12, shards, smp, shard_device)
+        finish_a()
+        finish_ranks_a = send_ranks(0, 0)
+        finish_b()
+        finish_ranks_b = send_ranks(0, 1)
     with jax.named_scope("shards"):
-        finish_shards[0]()
+        finish_shards()
         mine = by_shard[0]
         for source in range(1, shards):
             mine = mine + by_shard[source]
         by_total[grp] = mine
-        finish_total = gather(by_total, 9, groups, grp, group_device)
+        finish_total = gather(by_total, 13, groups, grp, group_device)
     with jax.named_scope("redr"):
-        finish_ranks()
-        values0, own_dot, _ = sum_ranks(0)
+        finish_ranks_a()
+        finish_ranks_b()
+        sums = [sum_ranks(0, side) for side in range(2)]
+        own_dot = sums[1][:, span : span + 1]
     with jax.named_scope("mean"):
         finish_total()
         mean0 = by_total[0]
         for source in range(1, groups):
             mean0 = mean0 + by_total[source]
-        centred = values0 - mean0[:, :1] / count
+        mean0 = mean0[:, :1] / count
+        centred = [whole[:, :span] - mean0 for whole in sums]
     with jax.named_scope("scaled"):
         for at in range(0, samples, 512):
-            weights = centred[:, at : at + 512]
+            weights = centred[at // span][:, at % span : at % span + 512]
             scaled[:pair, at : at + 512] = (spins[:, at : at + 512].astype(F32) * weights).astype(BF16)
             scaled[pair:, at : at + 512] = jnp.concatenate(
                 [weights, jnp.zeros((PAD - 1, 512), F32)], axis=0
@@ -411,13 +419,15 @@
         image_arrived(at, 4)
         image_arrived(at, 5)
         fill_lhs(at, image_all, image_b[0])
-        values_of(1, at, at + 1)
+        values_of(1, at, at + 1, 0)
+        if at < parts - 1:
+            values_of(1, at, at + 1, 1)
 
     def named(name, step, *at):
         with jax.named_scope(name):
             step(*at)
 
-    finish_moment = gather_sets(0, [total(centred * centred), own_dot])
+    finish_moment = gather_sets(0, [total(centred[0] * centred[0]) + total(centred[1] * centred[1]), own_dot])
 
     def image_step(at, carry):
         image_part(at)
@@ -430,7 +440,7 @@
 
     with jax.named_scope("image"):
         lax.fori_loop(0, parts, image_step, 0)
-    finish_bias = gather(image_b, 7, SETS, member, set_device)
+    finish_bias = gather(image_b, 11, SETS, member, set_device)
     named("core", sum_core, 3)
     named("sumz", sum_z, 0)
     named("sumz", sum_z, 1)
@@ -451,9 +461,9 @@
         image_b[0] = whole_b
     named("sumx", sum_x, 2)
     named("sharez", share_z, 0)
-    named("values1", image_values, 0)
     named("sumx", sum_x, 3)
     named("sharez", share_z, 1)
+    named("values1", image_values, 0)
     with jax.named_scope("norm"):
         residual_b = keep * force_b_ref[...] - pull * whole_b
         own_norm = total(residual_b * residual_b) / shards
@@ -468,23 +478,33 @@
             image_ref[:, cols_of(at)] = own
             own_ref[:, cols_of(at)] = force
         finish_norm = gather_sets(1, [own_norm, own_cross])
+    named("sharez", share_z, 2)
     named("values1", image_values, 1)
-    named("sharez", share_z, 2)
+    named("sharez", share_z, 3)
     named("values1", image_values, 2)
-    named("sharez", share_z, 3)
-    named("values1", image_values, 3)
     named("fnorm", finish_norm)
-
-    finish_ranks = sum_groups(1, set_sum(1, 0), set_sum(1, 1), lambda: None)
+    extras(1, set_sum(1, 0), set_sum(1, 1))
+    with jax.named_scope("values1"):
+        image_values(3)
+        finish_a = send_groups(1, 0)
+        values_of(1, parts - 1, parts, 1)
+        finish_b = send_groups(1, 1)
+    with jax.named_scope("redg"):
+        finish_a()
+        finish_ranks_a = send_ranks(1, 0)
+        finish_b()
+        finish_ranks_b = send_ranks(1, 1)
     with jax.named_scope("redr"):
-        finish_ranks()
-        values1, norm1, cross = sum_ranks(1)
+        finish_ranks_a()
+        finish_ranks_b()
+        sums = [sum_ranks(1, side) for side in range(2)]
+        norm1, cross = sums[1][:, span : span + 1], sums[1][:, span + 128 : span + 129]
     beta = norm1 / norm0
     with jax.named_scope("sets"):
-        values1 = (keep + beta) * centred - pull * values1
-        mean1 = total(values1) / samples
-        values1 = values1 - mean1
-        gather_sets(2, [mean1, total(values1 * values1)])()
+        values1 = [(keep + beta) * centred[side] - pull * sums[side][:, :span] for side in range(2)]
+        mean1 = (total(values1[0]) + total(values1[1])) / samples
+        values1 = [value - mean1 for value in values1]
+        gather_sets(2, [mean1, total(values1[0] * values1[0]) + total(values1[1] * values1[1])])()
         middle = set_sum(2, 0) / SETS
         spread = jnp.zeros((1, 1), F32)
         for source in range(SETS):
@@ -543,6 +563,7 @@
             pltpu.VMEM((units, 128), F32),
             pltpu.VMEM((1, units), F32),
             pltpu.VMEM((inputs, 2 * quarter), BF16),
+            pltpu.VMEM((inputs, 2 * quarter), BF16),
             pltpu.VMEM((pair, samples), BF16),
             pltpu.VMEM((units, samples), BF16),
             pltpu.VMEM((parts, 2, 2, 2, rows, PART), F32),
@@ -554,8 +575,10 @@
             pltpu.VMEM((parts, 2, rows, PART), F32),
             pltpu.VMEM((parts, 2, 2, 2, rows, PART), F32),
             pltpu.VMEM((SETS, 1, units), F32),
-            pltpu.VMEM((2, groups, 1, samples + EXTRA), F32),
-            pltpu.VMEM((2, ranks, 1, samples + EXTRA), F32),
+            pltpu.VMEM((2, groups, 1, samples // 2), F32),
+            pltpu.VMEM((2, groups, 1, samples // 2 + EXTRA), F32),
+            pltpu.VMEM((2, ranks, 1, samples // 2), F32),
+            pltpu.VMEM((2, ranks, 1, samples // 2 + EXTRA), F32),
             pltpu.VMEM((3, SETS, 8, 128), F32),
             pltpu.VMEM((shards, 1, 128), F32),
             pltpu.VMEM((groups, 1, 128), F32),
@@ -568,8 +591,8 @@
             dma((parts, 5)),
             dma((6,)),
             dma((parts, 6)),
-            dma((10,)),
-            dma((10,)),
+            dma((14,)),
+            dma((14,)),
         ],
         compiler_params=pltpu.CompilerParams(
             collective_id=0, has_side_effects=True, vmem_limit_bytes=62 * 1024 * 1024

time: 77.8 us -> 76.3 us (0.981)
  Pallas kernels: 77.1 us -> 75.5 us
    pallas_call x1, Pallas kernels: 76.4 us -> 74.8 us  [body(): pl.pallas_call(functools.partial(kernel, groups, shards), out_shape=(pltp...]
where the time goes in v4:
time: 76.3 us; the launch traced here: 76.2 us
  Pallas kernels  75.5 us (99%)
    pallas_call x1, Pallas kernels, body(): pl.pallas_call(functools.partial(kernel, groups, shards), out_shape=(pltp...  74.8 us

profile of v4, /device:TPU:1, one launch (start us, length us, event | category | flops | bytes accessed | tf_op | source)
XLA Modules:
  0.0 76.2 jit_solution(18407976483751237683)
XLA Ops:
  0.6 74.8 %shard_map.68 = (f32[32,1024]{1,0:T(8,128)S(1)}, f32[8,1024]{1,0:T(8,128)S(1)}, f32[32,1024]{1,0:T(8,128)S(1)}, f32[8,128]{1,0:T(8,128)S(1)}) custom-call(s32[32,1024]{1,0:T(8,128)} %packed_in.1, bf16[1024,1024]{1,0:T(8,128)(2,1)} %weight_in.1, f32[1,1024]{1,0:T(1,128)} %bitcast.3, f32[32,1024]{1,0:T(8,128)} %force_in.1, f32[1,1024]{1,0:T(1,128)} %bitcast.4), custom_call_target="tpu_custom_call" | custom-call | tf_op jit(solution)/shard_map/pallas_call | solution.py:550
  75.5 0.7 shard_map.69

commit v5 on v4

--- a/solution.py
+++ b/solution.py
@@ -25,7 +25,7 @@
     groups, shards,
     packed_in, weight_in, bias_in, force_in, force_b_in,
     image_ref, image_b_ref, own_ref, scale_ref,
-    packed, weight, weight_t, bias_ref, bias_t, force_b_ref, tile_a, tile_b, spins, hidden, force_all, lhs, scaled,
+    packed, weight, weight_t, bias_ref, bias_t, force_b_ref, tile, spins, hidden, force_all, lhs, scaled, plain,
     image, image_core, image_z, image_x, image_all, image_b, by_group_a, by_group_b, by_rank_a, by_rank_b, by_set, by_shard, by_total,
     load, spin_send, spin_recv, pass_send, pass_recv, force_send, force_recv, image_send, image_recv,
     gather_send, gather_recv,
@@ -178,7 +178,7 @@
     def places(pieces):
         return [pl.ds(pl.multiple_of(source * here + at * quarter, quarter), quarter) for source, at in pieces]
 
-    def unpack(tile, pieces):
+    def unpack(pieces):
         cols = places(pieces)
         for which, (source, at) in enumerate(pieces):
             to = slice(which * quarter, (which + 1) * quarter)
@@ -193,7 +193,7 @@
                     from_rows, which * quarter : (which + 1) * quarter
                 ]
 
-    def activate(tile, pieces):
+    def activate(pieces):
         cols = places(pieces)
         for unit in range(0, units, 512):
             these = pl.ds(unit, 512)
@@ -203,9 +203,13 @@
             for which in range(2):
                 hidden[these, cols[which]] = result[:, which * quarter : (which + 1) * quarter]
 
-    first, second = ((rank, 0), (rank, 1)), ((rank, 2), (rank, 3))
-    with jax.named_scope("unpack0"):
-        unpack(tile_a, first)
+    def hidden_of(*pieces):
+        unpack(pieces)
+        activate(pieces)
+
+    first = (rank, 0), (rank, 1)
+    spins[pair:, :] = (lax.broadcasted_iota(jnp.int32, (PAD, samples), 0) == 0).astype(F32).astype(BF16)
+    unpack(first)
     with jax.named_scope("barrier"):
         pl.semaphore_wait(barrier, groups + ranks + 1)
     for at in range(parts):
@@ -216,42 +220,37 @@
         force_send_own(at, 0, z_partner)
 
     with jax.named_scope("hidden0"):
-        unpack(tile_b, second)
-        activate(tile_a, first)
-    with jax.named_scope("hidden1"):
-        activate(tile_b, second)
+        activate(first)
+        hidden_of((rank, 2), (rank, 3))
     with jax.named_scope("spinab"):
         spin_arrived(before)
         hand_on(before, 0)
         spin_arrived(after)
         hand_on(after, 1)
+    with jax.named_scope("hidden1"):
+        hidden_of((before, y), (after, y))
+    with jax.named_scope("spin1"):
+        pieces = handed(before, 1), handed(after, 1)
     with jax.named_scope("hidden2"):
-        pieces = ((before, y), (after, y))
-        unpack(tile_a, pieces)
-        activate(tile_a, pieces)
+        hidden_of(*pieces)
     with jax.named_scope("spinc"):
         spin_arrived(across)
         hand_on(across, 2)
         for at in range(parts):
             force_x(at)
-        pieces = ((across, y), handed(before, 1))
-    with jax.named_scope("unpack3"):
-        unpack(tile_b, pieces)
-    now, later = tile_b, tile_a
+        pieces = (across, y), handed(before, 3)
+    with jax.named_scope("hidden3"):
+        hidden_of(*pieces)
     for step, ((source_a, from_a), (source_b, from_b)) in enumerate(
-        (((before, 3), (after, 1)), ((after, 3), (before, 2)), ((after, 2), (across, 1)), ((across, 3), (across, 2)))
+        (((after, 3), (before, 2)), ((after, 2), (across, 1)), ((across, 3), (across, 2)))
     ):
         with jax.named_scope("wait"):
-            if step >= 2:
-                force_z(2 * step - 4)
-                force_z(2 * step - 3)
-            coming = (handed(source_a, from_a), handed(source_b, from_b))
-        with jax.named_scope("hidden3"):
-            unpack(later, coming)
-            activate(now, pieces)
-        now, later, pieces = later, now, coming
-    with jax.named_scope("hidden4"):
-        activate(now, pieces)
+            if step >= 1:
+                force_z(2 * step - 2)
+                force_z(2 * step - 1)
+            pieces = handed(source_a, from_a), handed(source_b, from_b)
+        with jax.named_scope("hidden4"):
+            hidden_of(*pieces)
 
     span = samples // 2
     by_group, by_rank = (by_group_a, by_group_b), (by_rank_a, by_rank_b)
@@ -263,12 +262,12 @@
             [row[:, cols_of(at)] / ranks, jnp.zeros((PAD - 1, PART), F32)], axis=0
         ).astype(BF16)
 
-    def values_of(which, first, last, side):
+    def values_of(which, first, last, side, fresh):
         these, cols = slice(first * PART, last * PART), slice(side * span, (side + 1) * span)
         product = jnp.dot(lhs[:, these], hidden[these, cols], preferred_element_type=F32)
-        value = jnp.sum(product[:pair] * spins[:, cols].astype(F32), axis=0, keepdims=True) + product[pair : pair + 1]
+        value = jnp.sum(product[:pair] * spins[:pair, cols].astype(F32), axis=0, keepdims=True) + product[pair : pair + 1]
         mine = by_group[side].at[which, grp, :, :span]
-        mine[...] = value if first == 0 else mine[...] + value
+        mine[...] = value if fresh else mine[...] + value
 
     with jax.named_scope("forcew"):
         for at in range(parts):
@@ -321,6 +320,11 @@
     force_dot = total(force_b_ref[...] * force_b_ref[...]) / shards
     for at in range(parts):
         force_dot = force_dot + total(own_force(at) * own_force(at))
+    def of_hidden(left, at):
+        return lax.dot_general(
+            left[...], hidden[cols_ds(at), :], (((1,), (1,)), ((), ())), preferred_element_type=F32
+        )
+
     def extras(which, first, second):
         by_group[1][which, grp, :, span:] = jnp.concatenate([wide(first), wide(second)], axis=1)
 
@@ -328,14 +332,20 @@
         return total(by_group[side][0, grp, :, :span])
 
     with jax.named_scope("values0"):
-        values_of(0, 0, parts, 0)
+        values_of(0, 0, parts, 0, True)
         finish_a = send_groups(0, 0)
         extras(0, force_dot, jnp.zeros((1, 1), F32))
-        values_of(0, 0, parts, 1)
+        values_of(0, 0, parts, 1, True)
         finish_b = send_groups(0, 1)
     with jax.named_scope("redg"):
         by_shard[smp] = wide(own_sum(0) + own_sum(1))
         finish_shards = gather(by_shard, 12, shards, smp, shard_device)
+
+        def plain_part(at, carry):
+            plain[at] = of_hidden(spins, at)
+            return carry
+
+        lax.fori_loop(0, parts, plain_part, 0)
         finish_a()
         finish_ranks_a = send_ranks(0, 0)
         finish_b()
@@ -352,102 +362,133 @@
         finish_ranks_b()
         sums = [sum_ranks(0, side) for side in range(2)]
         own_dot = sums[1][:, span : span + 1]
+        mean_own = (total(sums[0][:, :span]) + total(sums[1][:, :span])) / samples
+        centred = [whole[:, :span] - mean_own for whole in sums]
+    with jax.named_scope("scaled"):
+        for at in range(0, samples, 512):
+            weights = centred[at // span][:, at % span : at % span + 512]
+            scaled[:pair, at : at + 512] = (spins[:pair, at : at + 512].astype(F32) * weights).astype(BF16)
+            scaled[pair:, at : at + 512] = jnp.concatenate(
+                [weights, jnp.zeros((PAD - 1, 512), F32)], axis=0
+            ).astype(BF16)
+
+    def outer(at):
+        return (x_partner, z_partner, half) if at % 2 == 0 else (z_partner, x_partner, parity)
+
+    def pick(ref, at, which):
+        return ref.at[:, which] if at % 2 == 0 else ref.at[which]
+
+    def core_copy(at):
+        return remote(image.at[at, 1 - core], image_core.at[at], image_send.at[0], image_recv.at[at, 0], sibling)
+
+    def image_copy(at, which):
+        far, near, place = outer(at)
+        ours = pick(image_all.at[at, core], at, place)
+        theirs = pick(image_all.at[at, core], at, 1 - place)
+        source, target, where = (
+            None,
+            (pick(image.at[at, core], at, 1 - place), image_z.at[at], far),
+            (pick(image.at[at, core], at, place), image_x.at[at], near),
+            (ours, ours, far),
+            (ours, ours, sibling),
+            (theirs, theirs, sibling),
+        )[which]
+        return remote(source, target, image_send.at[which], image_recv.at[at, which], where)
+
+    def image_arrived(at, which):
+        place = outer(at)[2]
+        target = (
+            image_core.at[at], image_z.at[at], image_x.at[at],
+            pick(image_all.at[at, core], at, 1 - place),
+            pick(image_all.at[at, 1 - core], at, place),
+            pick(image_all.at[at, 1 - core], at, 1 - place),
+        )[which]
+        remote(target, target, image_send.at[which], image_recv.at[at, which], sibling).wait_recv()
+
+    def image_part(at, carry):
+        part = of_hidden(scaled, at)
+        for to in range(SETS):
+            image[at, to // 4, to // 2 % 2, to % 2] = part[to * rows : (to + 1) * rows]
+        image_b[member, :, cols_ds(at)] = part[pair : pair + 1]
+        return carry
+
+    def shifted(at):
+        for to in range(SETS):
+            block = image.at[at, to // 4, to // 2 % 2, to % 2]
+            block[...] = block[...] + shift * plain[at, to * rows : (to + 1) * rows]
+        core_copy(at).start()
+        image_b[member, :, cols_ds(at)] = image_b[member, :, cols_ds(at)] + shift * plain[at, pair : pair + 1]
+
+    def sum_core(at):
+        place = outer(at)[2]
+        image_arrived(at, 0)
+        theirs = pick(image.at[at, core], at, 1 - place)
+        theirs[...] = theirs[...] + pick(image_core.at[at], at, 1 - place)[...]
+        image_copy(at, 1).start()
+        ours = pick(image.at[at, core], at, place)
+        ours[...] = ours[...] + pick(image_core.at[at], at, place)[...]
+
+    def sum_outer(at):
+        image_arrived(at, 1)
+        ours = pick(image.at[at, core], at, outer(at)[2])
+        ours[...] = ours[...] + image_z[at]
+        image_copy(at, 2).start()
+
+    def sum_inner(at):
+        image_arrived(at, 2)
+        place = outer(at)[2]
+        pick(image_all.at[at, core], at, place)[...] = pick(image.at[at, core], at, place)[...] + image_x[at]
+        image_copy(at, 3).start()
+        image_copy(at, 4).start()
+
+    def share(at):
+        image_arrived(at, 3)
+        image_copy(at, 5).start()
+
+    def image_values(at, fresh, *sides):
+        image_arrived(at, 4)
+        image_arrived(at, 5)
+        fill_lhs(at, image_all, image_b[0])
+        for side in sides:
+            values_of(1, at, at + 1, side, fresh)
+
+    def named(name, step, *at):
+        with jax.named_scope(name):
+            step(*at)
+
+    with jax.named_scope("image"):
+        lax.fori_loop(0, 2, image_part, 0)
     with jax.named_scope("mean"):
         finish_total()
         mean0 = by_total[0]
         for source in range(1, groups):
             mean0 = mean0 + by_total[source]
-        mean0 = mean0[:, :1] / count
-        centred = [whole[:, :span] - mean0 for whole in sums]
-    with jax.named_scope("scaled"):
-        for at in range(0, samples, 512):
-            weights = centred[at // span][:, at % span : at % span + 512]
-            scaled[:pair, at : at + 512] = (spins[:, at : at + 512].astype(F32) * weights).astype(BF16)
-            scaled[pair:, at : at + 512] = jnp.concatenate(
-                [weights, jnp.zeros((PAD - 1, 512), F32)], axis=0
-            ).astype(BF16)
-
-    def image_copy(at, which):
-        source, target, where = (
-            (image.at[at, 1 - core], image_core.at[at], sibling),
-            (image.at[at, core, 1 - parity], image_z.at[at], z_partner),
-            (image.at[at, core, parity], image_x.at[at], x_partner),
-            (image_all.at[at, core, parity], image_all.at[at, core, parity], z_partner),
-            (image_all.at[at, core, parity], image_all.at[at, core, parity], sibling),
-            (image_all.at[at, core, 1 - parity], image_all.at[at, core, 1 - parity], sibling),
-        )[which]
-        return remote(source, target, image_send.at[which], image_recv.at[at, which], where)
-
-    def image_arrived(at, which):
-        target = (
-            image_core.at[at], image_z.at[at], image_x.at[at],
-            image_all.at[at, core, 1 - parity], image_all.at[at, 1 - core, parity], image_all.at[at, 1 - core, 1 - parity],
-        )[which]
-        remote(target, target, image_send.at[which], image_recv.at[at, which], sibling).wait_recv()
-
-    def image_part(at):
-        part = lax.dot_general(
-            scaled[...], hidden[cols_ds(at), :], (((1,), (1,)), ((), ())), preferred_element_type=F32
-        )
-        for to in range(SETS):
-            image[at, to // 4, to // 2 % 2, to % 2] = part[to * rows : (to + 1) * rows]
-        image_copy(at, 0).start()
-        image_b[member, :, cols_ds(at)] = part[pair : pair + 1]
-
-    def sum_core(at):
-        image_arrived(at, 0)
-        image[at, core, 1 - parity] = image[at, core, 1 - parity] + image_core[at, 1 - parity]
-        image_copy(at, 1).start()
-        image[at, core, parity] = image[at, core, parity] + image_core[at, parity]
-
-    def sum_z(at):
-        image_arrived(at, 1)
-        image[at, core, parity] = image[at, core, parity] + image_z[at]
-        image_copy(at, 2).start()
-
-    def sum_x(at):
-        image_arrived(at, 2)
-        image_all[at, core, parity] = image[at, core, parity] + image_x[at]
-        image_copy(at, 3).start()
-        image_copy(at, 4).start()
-
-    def share_z(at):
-        image_arrived(at, 3)
-        image_copy(at, 5).start()
-
-    def image_values(at):
-        image_arrived(at, 4)
-        image_arrived(at, 5)
-        fill_lhs(at, image_all, image_b[0])
-        values_of(1, at, at + 1, 0)
-        if at < parts - 1:
-            values_of(1, at, at + 1, 1)
-
-    def named(name, step, *at):
-        with jax.named_scope(name):
-            step(*at)
-
-    finish_moment = gather_sets(0, [total(centred[0] * centred[0]) + total(centred[1] * centred[1]), own_dot])
+        shift = mean_own - mean0[:, :1] / count
+        shifted(0)
+        shifted(1)
+        moment = total(centred[0] * centred[0]) + total(centred[1] * centred[1]) + samples * shift * shift
+        finish_moment = gather_sets(0, [moment, own_dot])
 
     def image_step(at, carry):
-        image_part(at)
-
-        @pl.when(at > 0)
+        image_part(at, 0)
+        shifted(at)
+
+        @pl.when(at == 2)
         def _():
-            sum_core(at - 1)
+            sum_core(0)
+            sum_core(1)
 
         return carry
 
     with jax.named_scope("image"):
-        lax.fori_loop(0, parts, image_step, 0)
+        lax.fori_loop(2, parts, image_step, 0)
     finish_bias = gather(image_b, 11, SETS, member, set_device)
+    named("core", sum_core, 2)
     named("core", sum_core, 3)
-    named("sumz", sum_z, 0)
-    named("sumz", sum_z, 1)
-    named("sumz", sum_z, 2)
-    named("sumx", sum_x, 0)
-    named("sumz", sum_z, 3)
-    named("sumx", sum_x, 1)
+    named("outer", sum_outer, 1)
+    named("outer", sum_outer, 0)
+    named("outer", sum_outer, 2)
+    named("outer", sum_outer, 3)
     with jax.named_scope("bias"):
         finish_moment()
         finish_bias()
@@ -459,11 +500,10 @@
         for source in range(1, SETS):
             whole_b = whole_b + image_b[source]
         image_b[0] = whole_b
-    named("sumx", sum_x, 2)
-    named("sharez", share_z, 0)
-    named("sumx", sum_x, 3)
-    named("sharez", share_z, 1)
-    named("values1", image_values, 0)
+    named("inner", sum_inner, 0)
+    named("inner", sum_inner, 1)
+    named("inner", sum_inner, 2)
+    named("inner", sum_inner, 3)
     with jax.named_scope("norm"):
         residual_b = keep * force_b_ref[...] - pull * whole_b
         own_norm = total(residual_b * residual_b) / shards
@@ -478,16 +518,19 @@
             image_ref[:, cols_of(at)] = own
             own_ref[:, cols_of(at)] = force
         finish_norm = gather_sets(1, [own_norm, own_cross])
-    named("sharez", share_z, 2)
-    named("values1", image_values, 1)
-    named("sharez", share_z, 3)
-    named("values1", image_values, 2)
+    named("share", share, 1)
+    named("share", share, 0)
+    named("values1", image_values, 1, True, 0, 1)
+    named("share", share, 2)
+    named("values1", image_values, 0, False, 0, 1)
+    named("share", share, 3)
+    named("values1", image_values, 2, False, 0, 1)
     named("fnorm", finish_norm)
     extras(1, set_sum(1, 0), set_sum(1, 1))
     with jax.named_scope("values1"):
-        image_values(3)
+        image_values(3, False, 0)
         finish_a = send_groups(1, 0)
-        values_of(1, parts - 1, parts, 1)
+        values_of(1, 3, 4, 1, False)
         finish_b = send_groups(1, 1)
     with jax.named_scope("redg"):
         finish_a()
@@ -501,7 +544,7 @@
         norm1, cross = sums[1][:, span : span + 1], sums[1][:, span + 128 : span + 129]
     beta = norm1 / norm0
     with jax.named_scope("sets"):
-        values1 = [(keep + beta) * centred[side] - pull * sums[side][:, :span] for side in range(2)]
+        values1 = [(keep + beta) * (centred[side] + shift) - pull * sums[side][:, :span] for side in range(2)]
         mean1 = (total(values1[0]) + total(values1[1])) / samples
         values1 = [value - mean1 for value in values1]
         gather_sets(2, [mean1, total(values1[0] * values1[0]) + total(values1[1] * values1[1])])()
@@ -563,12 +606,12 @@
             pltpu.VMEM((units, 128), F32),
             pltpu.VMEM((1, units), F32),
             pltpu.VMEM((inputs, 2 * quarter), BF16),
-            pltpu.VMEM((inputs, 2 * quarter), BF16),
-            pltpu.VMEM((pair, samples), BF16),
+            pltpu.VMEM((pair + PAD, samples), BF16),
             pltpu.VMEM((units, samples), BF16),
             pltpu.VMEM((parts, 2, 2, 2, rows, PART), F32),
             pltpu.VMEM((pair + PAD, units), BF16),
             pltpu.VMEM((pair + PAD, samples), BF16),
+            pltpu.VMEM((parts, pair + PAD, PART), F32),
             pltpu.VMEM((parts, 2, 2, 2, rows, PART), F32),
             pltpu.VMEM((parts, 2, 2, rows, PART), F32),
             pltpu.VMEM((parts, 2, rows, PART), F32),

time: 76.3 us -> 75.4 us (0.988)
  Pallas kernels: 75.5 us -> 74.7 us
    pallas_call x1, Pallas kernels: 74.8 us -> 73.9 us  [body(): pl.pallas_call(functools.partial(kernel, groups, shards), out_shape=(pltp...]
where the time goes in v5:
time: 75.4 us; the launch traced here: 75.3 us
  Pallas kernels  74.7 us (99%)
    pallas_call x1, Pallas kernels, body(): pl.pallas_call(functools.partial(kernel, groups, shards), out_shape=(pltp...  73.9 us

profile of v5, /device:TPU:1, one launch (start us, length us, event | category | flops | bytes accessed | tf_op | source)
XLA Modules:
  0.0 75.3 jit_solution(17540281599115952344)
XLA Ops:
  0.6 73.9 %shard_map.68 = (f32[32,1024]{1,0:T(8,128)S(1)}, f32[8,1024]{1,0:T(8,128)S(1)}, f32[32,1024]{1,0:T(8,128)S(1)}, f32[8,128]{1,0:T(8,128)S(1)}) custom-call(s32[32,1024]{1,0:T(8,128)} %packed_in.1, bf16[1024,1024]{1,0:T(8,128)(2,1)} %weight_in.1, f32[1,1024]{1,0:T(1,128)} %bitcast.3, f32[32,1024]{1,0:T(8,128)} %force_in.1, f32[1,1024]{1,0:T(1,128)} %bitcast.4), custom_call_target="tpu_custom_call" | custom-call | tf_op jit(solution)/shard_map/pallas_call | solution.py:593
  74.6 0.7 shard_map.69

commit v6 on v5

--- a/solution.py
+++ b/solution.py
@@ -87,29 +87,25 @@
     def cols_ds(at):
         return pl.ds(pl.multiple_of(at * PART, PART), PART)
 
-    def load_all():
-        copies = [
-            pltpu.make_async_copy(weight_in, weight, load.at[0]),
-            pltpu.make_async_copy(bias_in, bias_ref, load.at[1]),
-            pltpu.make_async_copy(force_b_in, force_b_ref, load.at[2]),
-        ]
-        for at in range(LINE):
-            copies.append(
-                pltpu.make_async_copy(packed_in.at[:, pl.ds(at * quarter, quarter)], packed.at[rank, at], load.at[3])
-            )
-        for at in range(parts):
-            copies.append(
-                pltpu.make_async_copy(force_in.at[:, cols_ds(at)], force_all.at[at, core, parity, half], load.at[4])
-            )
-        for copy in copies:
-            copy.start()
-        for copy in copies[:3]:
-            copy.wait()
-        pltpu.make_async_copy(packed.at[rank], packed.at[rank], load.at[3]).wait()
-        blocks = force_all.at[:, core, parity, half]
-        pltpu.make_async_copy(blocks, blocks, load.at[4]).wait()
-
-    load_all()
+    copies = []
+    for at in range(LINE):
+        copies.append(
+            pltpu.make_async_copy(packed_in.at[:, pl.ds(at * quarter, quarter)], packed.at[rank, at], load.at[3])
+        )
+    for at in range(parts):
+        copies.append(
+            pltpu.make_async_copy(force_in.at[:, cols_ds(at)], force_all.at[at, core, parity, half], load.at[4])
+        )
+    later = [
+        pltpu.make_async_copy(weight_in, weight, load.at[0]),
+        pltpu.make_async_copy(bias_in, bias_ref, load.at[1]),
+        pltpu.make_async_copy(force_b_in, force_b_ref, load.at[2]),
+    ]
+    for copy in copies + later:
+        copy.start()
+    pltpu.make_async_copy(packed.at[rank], packed.at[rank], load.at[3]).wait()
+    blocks = force_all.at[:, core, parity, half]
+    pltpu.make_async_copy(blocks, blocks, load.at[4]).wait()
 
     def turn(at, carry):
         cols = pl.ds(pl.multiple_of(at * 256, 256), 256)
@@ -117,8 +113,6 @@
         bias_t[cols, :] = jnp.broadcast_to(bias_ref[:, cols], (128, 256)).T
         return carry
 
-    with jax.named_scope("turn"):
-        lax.fori_loop(0, units // 256, turn, 0)
     after, before, across = lax.rem(rank + 1, ranks), lax.rem(rank + ranks - 1, ranks), lax.rem(rank + 2, ranks)
 
     def force_send_own(at, which, where):
@@ -161,7 +155,7 @@
         remote(target, target, spin_send.at[0], spin_recv.at[source], sibling).wait_recv()
 
     def hand_on(source, slot):
-        for step in range(1, LINE):
+        for step in (1, 3, 2):
             piece = packed.at[source, y]
             remote(
                 piece, piece, pass_send.at[slot], pass_recv.at[source, y], line_device(lax.rem(y + step, LINE))
@@ -195,8 +189,8 @@
 
     def activate(pieces):
         cols = places(pieces)
-        for unit in range(0, units, 512):
-            these = pl.ds(unit, 512)
+        for unit in range(0, units, 1024):
+            these = pl.ds(unit, 1024)
             pre = jnp.dot(weight_t[these, :], tile[...], preferred_element_type=F32)
             pre = pre + jnp.concatenate([bias_t[these, :]] * (2 * quarter // 128), axis=1)
             result = jnp.tanh(pre).astype(BF16)
@@ -207,9 +201,6 @@
         unpack(pieces)
         activate(pieces)
 
-    first = (rank, 0), (rank, 1)
-    spins[pair:, :] = (lax.broadcasted_iota(jnp.int32, (PAD, samples), 0) == 0).astype(F32).astype(BF16)
-    unpack(first)
     with jax.named_scope("barrier"):
         pl.semaphore_wait(barrier, groups + ranks + 1)
     for at in range(parts):
@@ -219,8 +210,13 @@
     for at in range(parts):
         force_send_own(at, 0, z_partner)
 
+    spins[pair:, :] = (lax.broadcasted_iota(jnp.int32, (PAD, samples), 0) == 0).astype(F32).astype(BF16)
+    with jax.named_scope("turn"):
+        for copy in later:
+            copy.wait()
+        lax.fori_loop(0, units // 256, turn, 0)
     with jax.named_scope("hidden0"):
-        activate(first)
+        hidden_of((rank, 0), (rank, 1))
         hidden_of((rank, 2), (rank, 3))
     with jax.named_scope("spinab"):
         spin_arrived(before)
@@ -229,28 +225,26 @@
         hand_on(after, 1)
     with jax.named_scope("hidden1"):
         hidden_of((before, y), (after, y))
-    with jax.named_scope("spin1"):
-        pieces = handed(before, 1), handed(after, 1)
-    with jax.named_scope("hidden2"):
-        hidden_of(*pieces)
     with jax.named_scope("spinc"):
         spin_arrived(across)
         hand_on(across, 2)
         for at in range(parts):
             force_x(at)
-        pieces = (across, y), handed(before, 3)
+        pieces = (across, y), handed(before, 1)
+    with jax.named_scope("hidden2"):
+        hidden_of(*pieces)
+    with jax.named_scope("wait"):
+        pieces = handed(before, 3), handed(after, 1), handed(after, 3), handed(before, 2)
     with jax.named_scope("hidden3"):
-        hidden_of(*pieces)
-    for step, ((source_a, from_a), (source_b, from_b)) in enumerate(
-        (((after, 3), (before, 2)), ((after, 2), (across, 1)), ((across, 3), (across, 2)))
-    ):
-        with jax.named_scope("wait"):
-            if step >= 1:
-                force_z(2 * step - 2)
-                force_z(2 * step - 1)
-            pieces = handed(source_a, from_a), handed(source_b, from_b)
-        with jax.named_scope("hidden4"):
-            hidden_of(*pieces)
+        hidden_of(*pieces[:2])
+        hidden_of(*pieces[2:])
+    with jax.named_scope("wait"):
+        for at in range(parts):
+            force_z(at)
+        pieces = handed(after, 2), handed(across, 1), handed(across, 3), handed(across, 2)
+    with jax.named_scope("hidden4"):
+        hidden_of(*pieces[:2])
+        hidden_of(*pieces[2:])
 
     span = samples // 2
     by_group, by_rank = (by_group_a, by_group_b), (by_rank_a, by_rank_b)
@@ -445,12 +439,10 @@
         image_arrived(at, 3)
         image_copy(at, 5).start()
 
-    def image_values(at, fresh, *sides):
+    def image_ready(at):
         image_arrived(at, 4)
         image_arrived(at, 5)
         fill_lhs(at, image_all, image_b[0])
-        for side in sides:
-            values_of(1, at, at + 1, side, fresh)
 
     def named(name, step, *at):
         with jax.named_scope(name):
@@ -520,17 +512,22 @@
         finish_norm = gather_sets(1, [own_norm, own_cross])
     named("share", share, 1)
     named("share", share, 0)
-    named("values1", image_values, 1, True, 0, 1)
+    named("ready", image_ready, 1)
     named("share", share, 2)
-    named("values1", image_values, 0, False, 0, 1)
+    named("ready", image_ready, 0)
+    with jax.named_scope("values1"):
+        values_of(1, 0, 2, 0, True)
     named("share", share, 3)
-    named("values1", image_values, 2, False, 0, 1)
+    with jax.named_scope("values1"):
+        values_of(1, 0, 2, 1, True)
+    named("ready", image_ready, 2)
+    named("ready", image_ready, 3)
     named("fnorm", finish_norm)
     extras(1, set_sum(1, 0), set_sum(1, 1))
     with jax.named_scope("values1"):
-        image_values(3, False, 0)
+        values_of(1, 2, 4, 0, False)
         finish_a = send_groups(1, 0)
-        values_of(1, 3, 4, 1, False)
+        values_of(1, 2, 4, 1, False)
         finish_b = send_groups(1, 1)
     with jax.named_scope("redg"):
         finish_a()

time: 75.4 us -> 73.5 us (0.975)
  Pallas kernels: 74.7 us -> 72.8 us
    pallas_call x1, Pallas kernels: 73.9 us -> 72.1 us  [body(): pl.pallas_call(functools.partial(kernel, groups, shards), out_shape=(pltp...]
where the time goes in v6:
time: 73.5 us; the launch traced here: 73.4 us
  Pallas kernels  72.8 us (99%)
    pallas_call x1, Pallas kernels, body(): pl.pallas_call(functools.partial(kernel, groups, shards), out_shape=(pltp...  72.1 us

profile of v6, /device:TPU:1, one launch (start us, length us, event | category | flops | bytes accessed | tf_op | source)
XLA Modules:
  0.0 73.4 jit_solution(13378806229536416536)
XLA Ops:
  0.6 72.1 %shard_map.68 = (f32[32,1024]{1,0:T(8,128)S(1)}, f32[8,1024]{1,0:T(8,128)S(1)}, f32[32,1024]{1,0:T(8,128)S(1)}, f32[8,128]{1,0:T(8,128)S(1)}) custom-call(s32[32,1024]{1,0:T(8,128)} %packed_in.1, bf16[1024,1024]{1,0:T(8,128)(2,1)} %weight_in.1, f32[1,1024]{1,0:T(1,128)} %bitcast.3, f32[32,1024]{1,0:T(8,128)} %force_in.1, f32[1,1024]{1,0:T(1,128)} %bitcast.4), custom_call_target="tpu_custom_call" | custom-call | tf_op jit(solution)/shard_map/pallas_call | solution.py:590
  72.7 0.7 shard_map.69

commit v7 on v6

--- a/solution.py
+++ b/solution.py
@@ -14,6 +14,7 @@
 EXTRA = 256
 PAD = 16
 PART = 256
+PIECE = 128
 LINE = 4
 
 
@@ -40,6 +41,7 @@
     count = samples * SETS
     quarter = here // LINE
     parts = units // PART
+    pieces = units // PIECE
     depth = 2 * ranks
 
     core, z, half = lax.rem(smp, 2), lax.rem(smp // 2, depth), smp // (2 * depth)
@@ -169,12 +171,12 @@
 
     masks = jnp.left_shift(1, lax.broadcasted_iota(jnp.int32, (32, quarter), 0))
 
-    def places(pieces):
-        return [pl.ds(pl.multiple_of(source * here + at * quarter, quarter), quarter) for source, at in pieces]
-
-    def unpack(pieces):
-        cols = places(pieces)
-        for which, (source, at) in enumerate(pieces):
+    def places(tiles):
+        return [pl.ds(pl.multiple_of(source * here + at * quarter, quarter), quarter) for source, at in tiles]
+
+    def unpack(tiles):
+        cols = places(tiles)
+        for which, (source, at) in enumerate(tiles):
             to = slice(which * quarter, (which + 1) * quarter)
             for word in range(words):
                 bits = jnp.bitwise_and(jnp.broadcast_to(packed[source, at, word : word + 1, :], (32, quarter)), masks)
@@ -187,8 +189,8 @@
                     from_rows, which * quarter : (which + 1) * quarter
                 ]
 
-    def activate(pieces):
-        cols = places(pieces)
+    def activate(tiles):
+        cols = places(tiles)
         for unit in range(0, units, 1024):
             these = pl.ds(unit, 1024)
             pre = jnp.dot(weight_t[these, :], tile[...], preferred_element_type=F32)
@@ -197,9 +199,9 @@
             for which in range(2):
                 hidden[these, cols[which]] = result[:, which * quarter : (which + 1) * quarter]
 
-    def hidden_of(*pieces):
-        unpack(pieces)
-        activate(pieces)
+    def hidden_of(*tiles):
+        unpack(tiles)
+        activate(tiles)
 
     with jax.named_scope("barrier"):
         pl.semaphore_wait(barrier, groups + ranks + 1)
@@ -230,30 +232,32 @@
         hand_on(across, 2)
         for at in range(parts):
             force_x(at)
-        pieces = (across, y), handed(before, 1)
+        tiles = (across, y), handed(before, 1)
     with jax.named_scope("hidden2"):
-        hidden_of(*pieces)
+        hidden_of(*tiles)
     with jax.named_scope("wait"):
-        pieces = handed(before, 3), handed(after, 1), handed(after, 3), handed(before, 2)
+        tiles = handed(before, 3), handed(after, 1), handed(after, 3), handed(before, 2)
     with jax.named_scope("hidden3"):
-        hidden_of(*pieces[:2])
-        hidden_of(*pieces[2:])
+        hidden_of(*tiles[:2])
+        hidden_of(*tiles[2:])
     with jax.named_scope("wait"):
         for at in range(parts):
             force_z(at)
-        pieces = handed(after, 2), handed(across, 1), handed(across, 3), handed(across, 2)
+        tiles = handed(after, 2), handed(across, 1), handed(across, 3), handed(across, 2)
     with jax.named_scope("hidden4"):
-        hidden_of(*pieces[:2])
-        hidden_of(*pieces[2:])
+        hidden_of(*tiles[:2])
+        hidden_of(*tiles[2:])
 
     span = samples // 2
     by_group, by_rank = (by_group_a, by_group_b), (by_rank_a, by_rank_b)
 
     def fill_lhs(at, slots, row):
+        width = slots.shape[-1]
+        cols = slice(at * width, (at + 1) * width)
         for to in range(SETS):
-            lhs[to * rows : (to + 1) * rows, cols_of(at)] = slots[at, to // 4, to // 2 % 2, to % 2].astype(BF16)
-        lhs[pair:, cols_of(at)] = jnp.concatenate(
-            [row[:, cols_of(at)] / ranks, jnp.zeros((PAD - 1, PART), F32)], axis=0
+            lhs[to * rows : (to + 1) * rows, cols] = slots[at, to // 4, to // 2 % 2, to % 2].astype(BF16)
+        lhs[pair:, cols] = jnp.concatenate(
+            [row[:, cols] / ranks, jnp.zeros((PAD - 1, width), F32)], axis=0
         ).astype(BF16)
 
     def values_of(which, first, last, side, fresh):
@@ -278,6 +282,21 @@
 
         return finish
 
+    def gather_shards():
+        send, recv = gather_send.at[12], gather_recv.at[12]
+        for far in sorted(range(depth), key=lambda apart: -min(apart, depth - apart)):
+            for half_at in (1 - half, half):
+                for core_at in (1 - core, core):
+                    if far or half_at is not half or core_at is not core:
+                        where = device(half_at, lax.rem(z + far, depth), core_at)
+                        remote(by_shard.at[smp], by_shard.at[smp], send, recv, where).start()
+        others = by_shard.at[pl.ds(0, shards - 1)]
+
+        def finish():
+            remote(others, others, send, recv, sibling).wait()
+
+        return finish
+
     def wide(x, lanes=128):
         return jnp.broadcast_to(x, (1, lanes))
 
@@ -333,17 +352,18 @@
         finish_b = send_groups(0, 1)
     with jax.named_scope("redg"):
         by_shard[smp] = wide(own_sum(0) + own_sum(1))
-        finish_shards = gather(by_shard, 12, shards, smp, shard_device)
+        finish_shards = gather_shards()
 
         def plain_part(at, carry):
             plain[at] = of_hidden(spins, at)
             return carry
 
-        lax.fori_loop(0, parts, plain_part, 0)
+        lax.fori_loop(0, parts - 1, plain_part, 0)
         finish_a()
         finish_ranks_a = send_ranks(0, 0)
         finish_b()
         finish_ranks_b = send_ranks(0, 1)
+        lax.fori_loop(parts - 1, parts, plain_part, 0)
     with jax.named_scope("shards"):
         finish_shards()
         mine = by_shard[0]
@@ -399,18 +419,26 @@
         )[which]
         remote(target, target, image_send.at[which], image_recv.at[at, which], sibling).wait_recv()
 
+    per = PART // PIECE
+
     def image_part(at, carry):
         part = of_hidden(scaled, at)
         for to in range(SETS):
-            image[at, to // 4, to // 2 % 2, to % 2] = part[to * rows : (to + 1) * rows]
+            for which in range(per):
+                image[per * at + which, to // 4, to // 2 % 2, to % 2] = part[
+                    to * rows : (to + 1) * rows, which * PIECE : (which + 1) * PIECE
+                ]
         image_b[member, :, cols_ds(at)] = part[pair : pair + 1]
         return carry
 
     def shifted(at):
-        for to in range(SETS):
-            block = image.at[at, to // 4, to // 2 % 2, to % 2]
-            block[...] = block[...] + shift * plain[at, to * rows : (to + 1) * rows]
-        core_copy(at).start()
+        for which in range(per):
+            for to in range(SETS):
+                block = image.at[per * at + which, to // 4, to // 2 % 2, to % 2]
+                block[...] = block[...] + shift * plain[
+                    at, to * rows : (to + 1) * rows, which * PIECE : (which + 1) * PIECE
+                ]
+            core_copy(per * at + which).start()
         image_b[member, :, cols_ds(at)] = image_b[member, :, cols_ds(at)] + shift * plain[at, pair : pair + 1]
 
     def sum_core(at):
@@ -467,20 +495,19 @@
 
         @pl.when(at == 2)
         def _():
-            sum_core(0)
-            sum_core(1)
+            for piece in range(2 * per):
+                sum_core(piece)
 
         return carry
 
     with jax.named_scope("image"):
         lax.fori_loop(2, parts, image_step, 0)
     finish_bias = gather(image_b, 11, SETS, member, set_device)
-    named("core", sum_core, 2)
-    named("core", sum_core, 3)
-    named("outer", sum_outer, 1)
-    named("outer", sum_outer, 0)
-    named("outer", sum_outer, 2)
-    named("outer", sum_outer, 3)
+    turns = [at ^ 1 for at in range(pieces)]
+    for at in range(2 * per, pieces):
+        named("core", sum_core, at)
+    for at in turns:
+        named("outer", sum_outer, at)
     with jax.named_scope("bias"):
         finish_moment()
         finish_bias()
@@ -492,10 +519,8 @@
         for source in range(1, SETS):
             whole_b = whole_b + image_b[source]
         image_b[0] = whole_b
-    named("inner", sum_inner, 0)
-    named("inner", sum_inner, 1)
-    named("inner", sum_inner, 2)
-    named("inner", sum_inner, 3)
+    for at in range(pieces):
+        named("inner", sum_inner, at)
     with jax.named_scope("norm"):
         residual_b = keep * force_b_ref[...] - pull * whole_b
         own_norm = total(residual_b * residual_b) / shards
@@ -503,25 +528,30 @@
         image_b_ref[0:1, :] = whole_b
         image_b_ref[1:2, :] = force_b_ref[...]
         for at in range(parts):
-            force, own = own_force(at), image_all[at, core, parity, half]
-            residual = keep * force - pull * own
-            own_norm = own_norm + total(residual * residual)
-            own_cross = own_cross + total(residual * force)
-            image_ref[:, cols_of(at)] = own
-            own_ref[:, cols_of(at)] = force
+            own_ref[:, cols_of(at)] = own_force(at)
+        for at in range(pieces):
+            image_ref[:, at * PIECE : (at + 1) * PIECE] = image_all[at, core, parity, half]
+        residual = keep * own_ref[...] - pull * image_ref[...]
+        own_norm = own_norm + total(residual * residual)
+        own_cross = own_cross + total(residual * own_ref[...])
         finish_norm = gather_sets(1, [own_norm, own_cross])
-    named("share", share, 1)
-    named("share", share, 0)
-    named("ready", image_ready, 1)
-    named("share", share, 2)
-    named("ready", image_ready, 0)
+    near, last = turns[: pieces // 2], turns[pieces // 2 :]
+    for at in near:
+        named("share", share, at)
+    for at in near[:2]:
+        named("ready", image_ready, at)
+    for at in last[:2]:
+        named("share", share, at)
+    for at in near[2:]:
+        named("ready", image_ready, at)
     with jax.named_scope("values1"):
         values_of(1, 0, 2, 0, True)
-    named("share", share, 3)
+    for at in last[2:]:
+        named("share", share, at)
     with jax.named_scope("values1"):
         values_of(1, 0, 2, 1, True)
-    named("ready", image_ready, 2)
-    named("ready", image_ready, 3)
+    for at in last:
+        named("ready", image_ready, at)
     named("fnorm", finish_norm)
     extras(1, set_sum(1, 0), set_sum(1, 1))
     with jax.named_scope("values1"):
@@ -582,7 +612,7 @@
     rows = force_w.shape[0]
     ranks = shards // SETS
     samples, pair = ranks * here, SETS * rows
-    parts = units // PART
+    parts, pieces = units // PART, units // PIECE
     quarter = here // LINE
     vmem = pl.BlockSpec(memory_space=pltpu.VMEM)
     anywhere = pl.BlockSpec(memory_space=pl.ANY)
@@ -609,11 +639,11 @@
             pltpu.VMEM((pair + PAD, units), BF16),
             pltpu.VMEM((pair + PAD, samples), BF16),
             pltpu.VMEM((parts, pair + PAD, PART), F32),
-            pltpu.VMEM((parts, 2, 2, 2, rows, PART), F32),
-            pltpu.VMEM((parts, 2, 2, rows, PART), F32),
-            pltpu.VMEM((parts, 2, rows, PART), F32),
-            pltpu.VMEM((parts, 2, rows, PART), F32),
-            pltpu.VMEM((parts, 2, 2, 2, rows, PART), F32),
+            pltpu.VMEM((pieces, 2, 2, 2, rows, PIECE), F32),
+            pltpu.VMEM((pieces, 2, 2, rows, PIECE), F32),
+            pltpu.VMEM((pieces, 2, rows, PIECE), F32),
+            pltpu.VMEM((pieces, 2, rows, PIECE), F32),
+            pltpu.VMEM((pieces, 2, 2, 2, rows, PIECE), F32),
             pltpu.VMEM((SETS, 1, units), F32),
             pltpu.VMEM((2, groups, 1, samples // 2), F32),
             pltpu.VMEM((2, groups, 1, samples // 2 + EXTRA), F32),
@@ -630,7 +660,7 @@
             dma((5,)),
             dma((parts, 5)),
             dma((6,)),
-            dma((parts, 6)),
+            dma((pieces, 6)),
             dma((14,)),
             dma((14,)),
         ],

time: 73.5 us -> 72.3 us (0.984)
  Pallas kernels: 72.8 us -> 71.5 us
    pallas_call x1, Pallas kernels: 72.1 us -> 70.8 us  [body(): pl.pallas_call(functools.partial(kernel, groups, shards), out_shape=(pltp...]
where the time goes in v7:
time: 72.3 us; the launch traced here: 72.2 us
  Pallas kernels  71.5 us (99%)
    pallas_call x1, Pallas kernels, body(): pl.pallas_call(functools.partial(kernel, groups, shards), out_shape=(pltp...  70.8 us

profile of v7, /device:TPU:1, one launch (start us, length us, event | category | flops | bytes accessed | tf_op | source)
XLA Modules:
  0.0 72.2 jit_solution(14049478883305007648)
XLA Ops:
  0.6 70.8 %shard_map.68 = (f32[32,1024]{1,0:T(8,128)S(1)}, f32[8,1024]{1,0:T(8,128)S(1)}, f32[32,1024]{1,0:T(8,128)S(1)}, f32[8,128]{1,0:T(8,128)S(1)}) custom-call(s32[32,1024]{1,0:T(8,128)} %packed_in.1, bf16[1024,1024]{1,0:T(8,128)(2,1)} %weight_in.1, f32[1,1024]{1,0:T(1,128)} %bitcast.3, f32[32,1024]{1,0:T(8,128)} %force_in.1, f32[1,1024]{1,0:T(1,128)} %bitcast.4), custom_call_target="tpu_custom_call" | custom-call | tf_op jit(solution)/shard_map/pallas_call | solution.py:620
  71.4 0.7 shard_map.69

commit v8 on v7

--- a/solution.py
+++ b/solution.py
@@ -65,12 +65,6 @@
     def rank_device(at):
         return device(half, 2 * at + parity, core)
 
-    def set_device(at):
-        return device(lax.rem(at, 2), 2 * rank + lax.rem(at // 2, 2), at // 4)
-
-    def shard_device(at):
-        return {"smp": at}
-
     def remote(source, target, send, recv, where):
         return pltpu.make_async_remote_copy(
             source, target, send, recv, device_id=where, device_id_type=MESH
@@ -117,36 +111,21 @@
 
     after, before, across = lax.rem(rank + 1, ranks), lax.rem(rank + ranks - 1, ranks), lax.rem(rank + 2, ranks)
 
-    def force_send_own(at, which, where):
-        own = force_all.at[at, core, parity, half]
-        remote(own, own, force_send.at[which], force_recv.at[at, which], where).start()
-
-    def force_arrived(at, which):
+    def force_copy(which):
+        source, recv, where = (
+            (force_all.at[:, core, parity, half], 0, z_partner),
+            (force_all.at[:, core, parity, half], 1, x_partner),
+            (force_all.at[:, core, parity, 1 - half], 0, z_partner),
+            (force_all.at[:, core, parity], 2, sibling),
+            (force_all.at[:, core, 1 - parity], 2, sibling),
+        )[which]
+        return remote(source, source, force_send.at[which], force_recv.at[recv], where)
+
+    def force_arrived(which):
         target = (
-            force_all.at[at, core, 1 - parity, half],
-            force_all.at[at, core, parity, 1 - half],
-            force_all.at[at, core, 1 - parity, 1 - half],
-            force_all.at[at, 1 - core, parity],
-            force_all.at[at, 1 - core, 1 - parity],
+            force_all.at[:, core, 1 - parity], force_all.at[:, core, parity, 1 - half], force_all.at[:, 1 - core]
         )[which]
-        remote(target, target, force_send.at[which], force_recv.at[at, which], sibling).wait_recv()
-
-    def force_x(at):
-        force_arrived(at, 1)
-        block_x = force_all.at[at, core, parity, 1 - half]
-        remote(block_x, block_x, force_send.at[2], force_recv.at[at, 2], z_partner).start()
-        ours = force_all.at[at, core, parity]
-        remote(ours, ours, force_send.at[3], force_recv.at[at, 3], sibling).start()
-
-    def force_z(at):
-        force_arrived(at, 0)
-        force_arrived(at, 2)
-        theirs = force_all.at[at, core, 1 - parity]
-        remote(theirs, theirs, force_send.at[4], force_recv.at[at, 4], sibling).start()
-
-    def force_whole(at):
-        force_arrived(at, 3)
-        force_arrived(at, 4)
+        remote(target, target, force_send.at[which], force_recv.at[which], sibling).wait_recv()
 
     def spin_send_to(step):
         own = packed.at[rank, y]
@@ -205,12 +184,10 @@
 
     with jax.named_scope("barrier"):
         pl.semaphore_wait(barrier, groups + ranks + 1)
-    for at in range(parts):
-        force_send_own(at, 1, x_partner)
-    for step in (1, ranks - 1, 2):
+    force_copy(1).start()
+    for step in (2, 1, ranks - 1):
         spin_send_to(step).start()
-    for at in range(parts):
-        force_send_own(at, 0, z_partner)
+    force_copy(0).start()
 
     spins[pair:, :] = (lax.broadcasted_iota(jnp.int32, (PAD, samples), 0) == 0).astype(F32).astype(BF16)
     with jax.named_scope("turn"):
@@ -230,19 +207,20 @@
     with jax.named_scope("spinc"):
         spin_arrived(across)
         hand_on(across, 2)
-        for at in range(parts):
-            force_x(at)
-        tiles = (across, y), handed(before, 1)
+        force_arrived(1)
+        force_copy(2).start()
+        force_copy(3).start()
+        tiles = (across, y), handed(before, 3)
     with jax.named_scope("hidden2"):
         hidden_of(*tiles)
     with jax.named_scope("wait"):
-        tiles = handed(before, 3), handed(after, 1), handed(after, 3), handed(before, 2)
+        tiles = handed(after, 3), handed(before, 1), handed(after, 1), handed(before, 2)
     with jax.named_scope("hidden3"):
         hidden_of(*tiles[:2])
         hidden_of(*tiles[2:])
     with jax.named_scope("wait"):
-        for at in range(parts):
-            force_z(at)
+        force_arrived(0)
+        force_copy(4).start()
         tiles = handed(after, 2), handed(across, 1), handed(across, 3), handed(across, 2)
     with jax.named_scope("hidden4"):
         hidden_of(*tiles[:2])
@@ -268,13 +246,25 @@
         mine[...] = value if fresh else mine[...] + value
 
     with jax.named_scope("forcew"):
+        force_arrived(2)
         for at in range(parts):
-            force_whole(at)
             fill_lhs(at, force_all, force_b_ref)
-    def gather(slots, which, size, me, peer):
+    other_groups = [
+        {"grp": (1 - column if across_x else column) * LINE + lax.rem(y + step, LINE)}
+        for across_x, step in ((1, 2), (0, 2), (1, 1), (1, 3), (0, 1), (0, 3), (1, 0))
+    ]
+    other_ranks = [rank_device(lax.rem(rank + step, ranks)) for step in (2, 1, 3)]
+    other_sets = [
+        device(half_at, z_at, core_at)
+        for half_at in (1 - half, half)
+        for z_at in (z + 1 - 2 * parity, z)
+        for core_at in (1 - core, core)
+    ][:-1]
+
+    def gather(slots, which, size, me, peers):
         send, recv = gather_send.at[which], gather_recv.at[which]
-        for step in range(1, size):
-            remote(slots.at[me], slots.at[me], send, recv, peer(lax.rem(me + step, size))).start()
+        for peer in peers:
+            remote(slots.at[me], slots.at[me], send, recv, peer).start()
         others = slots.at[pl.ds(0, size - 1)]
 
         def finish():
@@ -301,14 +291,14 @@
         return jnp.broadcast_to(x, (1, lanes))
 
     def send_groups(which, side):
-        return gather(by_group[side].at[which], 2 * which + side, groups, grp, group_device)
+        return gather(by_group[side].at[which], 2 * which + side, groups, grp, other_groups)
 
     def send_ranks(which, side):
         mine = by_group[side][which, 0]
         for source in range(1, groups):
             mine = mine + by_group[side][which, source]
         by_rank[side][which, rank] = mine
-        return gather(by_rank[side].at[which], 4 + 2 * which + side, ranks, rank, rank_device)
+        return gather(by_rank[side].at[which], 4 + 2 * which + side, ranks, rank, other_ranks)
 
     def sum_ranks(which, side):
         whole = by_rank[side][which, 0]
@@ -316,16 +306,15 @@
             whole = whole + by_rank[side][which, source]
         return whole
 
-    def gather_sets(which, values):
-        fill = jnp.zeros((8 - len(values), 128), F32)
-        by_set[which, member] = jnp.concatenate([wide(value) for value in values] + [fill], axis=0)
-        return gather(by_set.at[which], 8 + which, SETS, member, set_device)
+    def gather_sets(which, first, second):
+        by_set[which, member] = jnp.concatenate([wide(first, 64), wide(second, 64)], axis=1)
+        return gather(by_set.at[which], 8 + which, SETS, member, other_sets)
 
     def set_sum(which, row):
-        value = by_set[which, 0, row : row + 1, :]
+        value = by_set[which, 0]
         for source in range(1, SETS):
-            value = value + by_set[which, source, row : row + 1, :]
-        return value[:, :1]
+            value = value + by_set[which, source]
+        return value[:, 64 * row : 64 * row + 1]
 
     def own_force(at):
         return force_all[at, core, parity, half]
@@ -370,7 +359,7 @@
         for source in range(1, shards):
             mine = mine + by_shard[source]
         by_total[grp] = mine
-        finish_total = gather(by_total, 13, groups, grp, group_device)
+        finish_total = gather(by_total, 13, groups, grp, other_groups)
     with jax.named_scope("redr"):
         finish_ranks_a()
         finish_ranks_b()
@@ -407,15 +396,14 @@
             (ours, ours, sibling),
             (theirs, theirs, sibling),
         )[which]
-        return remote(source, target, image_send.at[which], image_recv.at[at, which], where)
+        return remote(source, target, image_send.at[which], image_recv.at[at, min(which, 4)], where)
 
     def image_arrived(at, which):
         place = outer(at)[2]
         target = (
             image_core.at[at], image_z.at[at], image_x.at[at],
             pick(image_all.at[at, core], at, 1 - place),
-            pick(image_all.at[at, 1 - core], at, place),
-            pick(image_all.at[at, 1 - core], at, 1 - place),
+            image_all.at[at, 1 - core],
         )[which]
         remote(target, target, image_send.at[which], image_recv.at[at, which], sibling).wait_recv()
 
@@ -469,7 +457,6 @@
 
     def image_ready(at):
         image_arrived(at, 4)
-        image_arrived(at, 5)
         fill_lhs(at, image_all, image_b[0])
 
     def named(name, step, *at):
@@ -487,7 +474,7 @@
         shifted(0)
         shifted(1)
         moment = total(centred[0] * centred[0]) + total(centred[1] * centred[1]) + samples * shift * shift
-        finish_moment = gather_sets(0, [moment, own_dot])
+        finish_moment = gather_sets(0, moment, own_dot)
 
     def image_step(at, carry):
         image_part(at, 0)
@@ -502,7 +489,7 @@
 
     with jax.named_scope("image"):
         lax.fori_loop(2, parts, image_step, 0)
-    finish_bias = gather(image_b, 11, SETS, member, set_device)
+    finish_bias = gather(image_b, 11, SETS, member, other_sets)
     turns = [at ^ 1 for at in range(pieces)]
     for at in range(2 * per, pieces):
         named("core", sum_core, at)
@@ -534,7 +521,7 @@
         residual = keep * own_ref[...] - pull * image_ref[...]
         own_norm = own_norm + total(residual * residual)
         own_cross = own_cross + total(residual * own_ref[...])
-        finish_norm = gather_sets(1, [own_norm, own_cross])
+        finish_norm = gather_sets(1, own_norm, own_cross)
     near, last = turns[: pieces // 2], turns[pieces // 2 :]
     for at in near:
         named("share", share, at)
@@ -574,11 +561,11 @@
         values1 = [(keep + beta) * (centred[side] + shift) - pull * sums[side][:, :span] for side in range(2)]
         mean1 = (total(values1[0]) + total(values1[1])) / samples
         values1 = [value - mean1 for value in values1]
-        gather_sets(2, [mean1, total(values1[0] * values1[0]) + total(values1[1] * values1[1])])()
+        gather_sets(2, mean1, total(values1[0] * values1[0]) + total(values1[1] * values1[1]))()
         middle = set_sum(2, 0) / SETS
         spread = jnp.zeros((1, 1), F32)
         for source in range(SETS):
-            shift = by_set[2, source, 0:1, :1] - middle
+            shift = by_set[2, source][:, :1] - middle
             spread = spread + shift * shift
         variance1 = (set_sum(2, 1) + samples * spread) / count
     direction_dot = norm1 + 2.0 * beta * cross + beta * beta * norm0
@@ -593,8 +580,7 @@
         for slot in range(3):
             remote(pieces, pieces, pass_send.at[slot], spin_recv.at[0], sibling).wait_send()
         for which in range(5):
-            blocks = force_all.at[:, core, parity] if which > 2 else force_all.at[:, core, parity, half]
-            remote(blocks, blocks, force_send.at[which], spin_recv.at[0], sibling).wait_send()
+            force_copy(which).wait_send()
         for which in range(6):
             blocks = image_core if which == 0 else image_z
             remote(blocks, blocks, image_send.at[which], spin_recv.at[0], sibling).wait_send()
@@ -649,7 +635,7 @@
             pltpu.VMEM((2, groups, 1, samples // 2 + EXTRA), F32),
             pltpu.VMEM((2, ranks, 1, samples // 2), F32),
             pltpu.VMEM((2, ranks, 1, samples // 2 + EXTRA), F32),
-            pltpu.VMEM((3, SETS, 8, 128), F32),
+            pltpu.VMEM((3, SETS, 1, 128), F32),
             pltpu.VMEM((shards, 1, 128), F32),
             pltpu.VMEM((groups, 1, 128), F32),
             dma((5,)),
@@ -658,9 +644,9 @@
             dma((3,)),
             dma((ranks, LINE)),
             dma((5,)),
-            dma((parts, 5)),
+            dma((3,)),
             dma((6,)),
-            dma((pieces, 6)),
+            dma((pieces, 5)),
             dma((14,)),
             dma((14,)),
         ],

time: 72.3 us -> 72.7 us (level)
  no operation moved by 1% of the time
where the time goes in v8:
time: 72.7 us; the launch traced here: 72.6 us
  Pallas kernels  72 us (99%)
    pallas_call x1, Pallas kernels, body(): pl.pallas_call(functools.partial(kernel, groups, shards), out_shape=(pltp...  71.3 us

profile of v8, /device:TPU:1, one launch (start us, length us, event | category | flops | bytes accessed | tf_op | source)
XLA Modules:
  0.0 72.6 jit_solution(3503190976897285667)
XLA Ops:
  0.6 71.3 %shard_map.68 = (f32[32,1024]{1,0:T(8,128)S(1)}, f32[8,1024]{1,0:T(8,128)S(1)}, f32[32,1024]{1,0:T(8,128)S(1)}, f32[8,128]{1,0:T(8,128)S(1)}) custom-call(s32[32,1024]{1,0:T(8,128)} %packed_in.1, bf16[1024,1024]{1,0:T(8,128)(2,1)} %weight_in.1, f32[1,1024]{1,0:T(1,128)} %bitcast.3, f32[32,1024]{1,0:T(8,128)} %force_in.1, f32[1,1024]{1,0:T(1,128)} %bitcast.4), custom_call_target="tpu_custom_call" | custom-call | tf_op jit(solution)/shard_map/pallas_call | solution.py:606
  71.9 0.7 shard_map.69

commit v9 on v8

--- a/solution.py
+++ b/solution.py
@@ -71,10 +71,10 @@
         )
 
     barrier = pltpu.get_barrier_semaphore()
-    for size, me, peer in ((groups, grp, group_device), (ranks, rank, rank_device)):
-        for step in range(1, size):
-            pl.semaphore_signal(barrier, device_id=peer(lax.rem(me + step, size)), device_id_type=MESH)
-    for where in (sibling, z_partner, x_partner):
+    greeted = [line_device(lax.rem(y + step, LINE)) for step in range(1, LINE)]
+    greeted += [group_device((1 - column) * LINE + y), sibling, z_partner, x_partner]
+    greeted += [rank_device(lax.rem(rank + step, ranks)) for step in (1, ranks - 1)]
+    for where in greeted:
         pl.semaphore_signal(barrier, device_id=where, device_id_type=MESH)
 
     def cols_of(at):
@@ -183,9 +183,9 @@
         activate(tiles)
 
     with jax.named_scope("barrier"):
-        pl.semaphore_wait(barrier, groups + ranks + 1)
+        pl.semaphore_wait(barrier, len(greeted))
     force_copy(1).start()
-    for step in (2, 1, ranks - 1):
+    for step in (1, ranks - 1):
         spin_send_to(step).start()
     force_copy(0).start()
 
@@ -199,6 +199,8 @@
         hidden_of((rank, 2), (rank, 3))
     with jax.named_scope("spinab"):
         spin_arrived(before)
+        relayed = packed.at[before, y]
+        remote(relayed, relayed, spin_send.at[0], spin_recv.at[before], rank_device(after)).start()
         hand_on(before, 0)
         spin_arrived(after)
         hand_on(after, 1)
@@ -249,17 +251,14 @@
         force_arrived(2)
         for at in range(parts):
             fill_lhs(at, force_all, force_b_ref)
-    other_groups = [
-        {"grp": (1 - column if across_x else column) * LINE + lax.rem(y + step, LINE)}
-        for across_x, step in ((1, 2), (0, 2), (1, 1), (1, 3), (0, 1), (0, 3), (1, 0))
-    ]
-    other_ranks = [rank_device(lax.rem(rank + step, ranks)) for step in (2, 1, 3)]
+    other_groups = [group_device(lax.rem(grp + step, groups)) for step in range(1, groups)]
+    other_ranks = [rank_device(lax.rem(rank + step, ranks)) for step in range(1, ranks)]
     other_sets = [
         device(half_at, z_at, core_at)
-        for half_at in (1 - half, half)
-        for z_at in (z + 1 - 2 * parity, z)
-        for core_at in (1 - core, core)
-    ][:-1]
+        for core_at in (core, 1 - core)
+        for z_at in (z, z + 1 - 2 * parity)
+        for half_at in (half, 1 - half)
+    ][1:]
 
     def gather(slots, which, size, me, peers):
         send, recv = gather_send.at[which], gather_recv.at[which]
@@ -307,14 +306,14 @@
         return whole
 
     def gather_sets(which, first, second):
-        by_set[which, member] = jnp.concatenate([wide(first, 64), wide(second, 64)], axis=1)
+        by_set[which, member] = jnp.concatenate([wide(first), wide(second), jnp.zeros((6, 128), F32)], axis=0)
         return gather(by_set.at[which], 8 + which, SETS, member, other_sets)
 
     def set_sum(which, row):
-        value = by_set[which, 0]
+        value = by_set[which, 0, row : row + 1, :]
         for source in range(1, SETS):
-            value = value + by_set[which, source]
-        return value[:, 64 * row : 64 * row + 1]
+            value = value + by_set[which, source, row : row + 1, :]
+        return value[:, :1]
 
     def own_force(at):
         return force_all[at, core, parity, half]
@@ -347,12 +346,12 @@
             plain[at] = of_hidden(spins, at)
             return carry
 
-        lax.fori_loop(0, parts - 1, plain_part, 0)
+        lax.fori_loop(0, 1, plain_part, 0)
         finish_a()
         finish_ranks_a = send_ranks(0, 0)
         finish_b()
         finish_ranks_b = send_ranks(0, 1)
-        lax.fori_loop(parts - 1, parts, plain_part, 0)
+        lax.fori_loop(1, 2, plain_part, 0)
     with jax.named_scope("shards"):
         finish_shards()
         mine = by_shard[0]
@@ -361,6 +360,7 @@
         by_total[grp] = mine
         finish_total = gather(by_total, 13, groups, grp, other_groups)
     with jax.named_scope("redr"):
+        lax.fori_loop(2, parts, plain_part, 0)
         finish_ranks_a()
         finish_ranks_b()
         sums = [sum_ranks(0, side) for side in range(2)]
@@ -565,7 +565,7 @@
         middle = set_sum(2, 0) / SETS
         spread = jnp.zeros((1, 1), F32)
         for source in range(SETS):
-            shift = by_set[2, source][:, :1] - middle
+            shift = by_set[2, source, 0:1, :1] - middle
             spread = spread + shift * shift
         variance1 = (set_sum(2, 1) + samples * spread) / count
     direction_dot = norm1 + 2.0 * beta * cross + beta * beta * norm0
@@ -635,7 +635,7 @@
             pltpu.VMEM((2, groups, 1, samples // 2 + EXTRA), F32),
             pltpu.VMEM((2, ranks, 1, samples // 2), F32),
             pltpu.VMEM((2, ranks, 1, samples // 2 + EXTRA), F32),
-            pltpu.VMEM((3, SETS, 1, 128), F32),
+            pltpu.VMEM((3, SETS, 8, 128), F32),
             pltpu.VMEM((shards, 1, 128), F32),
             pltpu.VMEM((groups, 1, 128), F32),
             dma((5,)),

time: 72.7 us -> 71.8 us (0.988)
  Pallas kernels: 72 us -> 71 us
    pallas_call x1, Pallas kernels: 71.3 us -> 70.3 us  [body(): pl.pallas_call(functools.partial(kernel, groups, shards), out_shape=(pltp...]
where the time goes in v9:
time: 71.8 us; the launch traced here: 71.7 us
  Pallas kernels  71 us (99%)
    pallas_call x1, Pallas kernels, body(): pl.pallas_call(functools.partial(kernel, groups, shards), out_shape=(pltp...  70.3 us

profile of v9, /device:TPU:1, one launch (start us, length us, event | category | flops | bytes accessed | tf_op | source)
XLA Modules:
  0.0 71.7 jit_solution(15329031840896240355)
XLA Ops:
  0.6 70.3 %shard_map.68 = (f32[32,1024]{1,0:T(8,128)S(1)}, f32[8,1024]{1,0:T(8,128)S(1)}, f32[32,1024]{1,0:T(8,128)S(1)}, f32[8,128]{1,0:T(8,128)S(1)}) custom-call(s32[32,1024]{1,0:T(8,128)} %packed_in.1, bf16[1024,1024]{1,0:T(8,128)(2,1)} %weight_in.1, f32[1,1024]{1,0:T(1,128)} %bitcast.3, f32[32,1024]{1,0:T(8,128)} %force_in.1, f32[1,1024]{1,0:T(1,128)} %bitcast.4), custom_call_target="tpu_custom_call" | custom-call | tf_op jit(solution)/shard_map/pallas_call | solution.py:606
  70.9 0.7 shard_map.69

commit v10 on v9

--- a/solution.py
+++ b/solution.py
@@ -206,17 +206,17 @@
         hand_on(after, 1)
     with jax.named_scope("hidden1"):
         hidden_of((before, y), (after, y))
+    with jax.named_scope("wait"):
+        tiles = handed(before, 3), handed(after, 3)
+    with jax.named_scope("hidden2"):
+        hidden_of(*tiles)
     with jax.named_scope("spinc"):
         spin_arrived(across)
         hand_on(across, 2)
         force_arrived(1)
         force_copy(2).start()
         force_copy(3).start()
-        tiles = (across, y), handed(before, 3)
-    with jax.named_scope("hidden2"):
-        hidden_of(*tiles)
-    with jax.named_scope("wait"):
-        tiles = handed(after, 3), handed(before, 1), handed(after, 1), handed(before, 2)
+        tiles = (across, y), handed(before, 1), handed(after, 1), handed(before, 2)
     with jax.named_scope("hidden3"):
         hidden_of(*tiles[:2])
         hidden_of(*tiles[2:])
@@ -346,12 +346,11 @@
             plain[at] = of_hidden(spins, at)
             return carry
 
-        lax.fori_loop(0, 1, plain_part, 0)
+        lax.fori_loop(0, 2, plain_part, 0)
         finish_a()
         finish_ranks_a = send_ranks(0, 0)
         finish_b()
         finish_ranks_b = send_ranks(0, 1)
-        lax.fori_loop(1, 2, plain_part, 0)
     with jax.named_scope("shards"):
         finish_shards()
         mine = by_shard[0]

time: 71.8 us -> 73.2 us (1.019)
  Pallas kernels: 71 us -> 72.4 us
    pallas_call x1, Pallas kernels: 70.3 us -> 71.7 us  [body(): pl.pallas_call(functools.partial(kernel, groups, shards), out_shape=(pltp...]
where the time goes in v10:
time: 73.2 us; the launch traced here: 73.1 us
  Pallas kernels  72.4 us (99%)
    pallas_call x1, Pallas kernels, body(): pl.pallas_call(functools.partial(kernel, groups, shards), out_shape=(pltp...  71.7 us

profile of v10, /device:TPU:1, one launch (start us, length us, event | category | flops | bytes accessed | tf_op | source)
XLA Modules:
  0.0 73.1 jit_solution(9457495387533737632)
XLA Ops:
  0.6 71.7 %shard_map.68 = (f32[32,1024]{1,0:T(8,128)S(1)}, f32[8,1024]{1,0:T(8,128)S(1)}, f32[32,1024]{1,0:T(8,128)S(1)}, f32[8,128]{1,0:T(8,128)S(1)}) custom-call(s32[32,1024]{1,0:T(8,128)} %packed_in.1, bf16[1024,1024]{1,0:T(8,128)(2,1)} %weight_in.1, f32[1,1024]{1,0:T(1,128)} %bitcast.3, f32[32,1024]{1,0:T(8,128)} %force_in.1, f32[1,1024]{1,0:T(1,128)} %bitcast.4), custom_call_target="tpu_custom_call" | custom-call | tf_op jit(solution)/shard_map/pallas_call | solution.py:605
  72.3 0.7 shard_map.69
